TPU v7x, 512 devices: a whole 4x8x8 slice. The times are simulated.
512 devices in a mesh: dp: 64 (over x, y, core), head: 8 (over z).
Axes of the slice: x: 4, y: 8, z: 8, core: 2. Of those that a mesh axis runs over, the one named last changes fastest.
Arguments:
- features: bfloat16 [2, 512, 196, 1024], P(None, ('dp', 'head'))
- patch_mask: int32 [2, 512, 196], P(None, ('dp', 'head')), may hold values from 0 to 1, as said below
- w_first: bfloat16 [1024, 2048], P('dp'), may hold values from -0.1875 to 0.1875
- w_second: bfloat16 [2048, 256], P('dp'), may hold values from -0.125 to 0.125
- proto_weight: bfloat16 [256, 8192], P('dp', 'head'), may hold values from -6 to 6
- center: float32 [8192], replicated, may hold values from -0.04 to 0.04
Outputs:
- targets: bfloat16 [2, 50176, 8192], P(None, ('dp', 'head'))
- new_center: float32 [8192], P('head')
Inputs may be any that keep to these rules, and one draw needn't show every extreme that they name: `patch_mask`: in each view every image masks between 19 and 98 of its patches, so that a block of 1 images fills at most 98 slots; in every draw the images of some block fill all 98 slots.
All inputs are finite; a program needn't handle non-finite values.
Results may differ from a plain program's by a relative error of at most 0.0086.
Values may be sent and summed in bfloat16 or wider, within the bound.
A program may use at most 64 MiB of HBM per device.

v0:
```python
import jax
import jax.numpy as jnp
from jax import lax
from jax.sharding import PartitionSpec as P

teacher_temp = 0.04
center_momentum = 0.9


def in_order(blocks, dim):
    blocks = jnp.moveaxis(blocks, 0, dim)
    dims = blocks.shape
    return blocks.reshape(*dims[:dim], dims[dim] * dims[dim + 1], *dims[dim + 2 :])


def from_everyone(x, axis):
    length = lax.axis_size(axis)
    return lax.all_to_all(jnp.broadcast_to(x[None], (length, *x.shape)), axis, 0, 0, tiled=True)


def collect(x, axis, dim):
    return in_order(from_everyone(x, axis), dim)


def of_everyone(x, axis):
    return from_everyone(x, axis).sum(axis=0)


def in_one(arrays, axis):
    ends = [0]
    for a in arrays:
        ends.append(ends[-1] + a.size)
    so_far = of_everyone(jnp.concatenate([a.ravel() for a in arrays]), axis)
    return tuple((so_far[b:e].reshape(a.shape) for a, b, e in zip(arrays, ends, ends[1:])))


def pack_rows(features, patch_mask):
    views, images, patches, width = features.shape
    capacity = images * (patches // 2)
    flat_feats = features.reshape(views, images * patches, width)
    flat_mask = patch_mask.reshape(views, images * patches)
    packed = []
    filled = []
    for view in range(views):
        places = jnp.nonzero(flat_mask[view], size=capacity, fill_value=0)[0].astype(jnp.int32)
        live = jnp.arange(capacity, dtype=jnp.int32) < jnp.sum(flat_mask[view])
        picked = jnp.take(flat_feats[view], places, axis=0)
        packed.append(jnp.where(live[:, None], picked, jnp.zeros((), picked.dtype)))
        filled.append(live)
    return (jnp.stack(packed), jnp.stack(filled))


def shards(features, patch_mask, w_first, w_second, proto_weight, center):
    groups = lax.axis_size("head")
    member = lax.axis_index("head")
    rows, live = pack_rows(features, patch_mask)
    views, capacity, width = rows.shape
    stacked = rows.reshape(views * capacity, width)
    hidden_width = w_first.shape[1]
    bottle_width = w_second.shape[1]
    begin = jnp.zeros((views * capacity, hidden_width), jnp.float32)
    piece = lax.all_gather(w_first, "dp", axis=0, tiled=True)
    part = lax.slice_in_dim(stacked, 0, piece.shape[0], axis=1)
    pre = begin + jnp.dot(part, piece, preferred_element_type=jnp.float32)
    hidden = jax.nn.gelu(pre, approximate=False).astype(jnp.bfloat16)
    start_sum = jnp.zeros((views * capacity, bottle_width), jnp.float32)
    part = hidden
    projected = start_sum + jnp.dot(
        part, collect(w_second, "dp", 0), preferred_element_type=jnp.float32
    )
    scale = lax.rsqrt(jnp.sum(projected * projected, axis=-1, keepdims=True) + 1e-06)
    normed = (projected * scale).astype(jnp.bfloat16).reshape(views, capacity, bottle_width)
    columns = collect(proto_weight, "dp", 0).astype(jnp.float32)
    local_protos = (
        columns * lax.rsqrt(jnp.sum(columns * columns, axis=0, keepdims=True) + 1e-06)
    ).astype(jnp.bfloat16)
    share_protos = local_protos.shape[1]
    total_protos = share_protos * groups
    results = []
    current = lax.dynamic_slice_in_dim(center, member * share_protos, share_protos, 0)
    for view in range(views):
        logits = jnp.dot(
            collect(normed[view], "head", 0), local_protos, preferred_element_type=jnp.float32
        )
        filled = jnp.any(logits != 0.0, axis=1)
        exps = jnp.exp((logits - current) / teacher_temp)
        totals = of_everyone(jnp.sum(exps, axis=1), "head")
        probs = total_protos * exps / totals[:, None]
        shares = jnp.where(filled[:, None], probs, jnp.zeros((), jnp.float32)).astype(jnp.bfloat16)
        results.append(lax.all_to_all(shares, "head", split_axis=0, concat_axis=1, tiled=True))
        sums, count = in_one((jnp.sum(logits, axis=0), jnp.sum(filled.astype(jnp.float32))), "dp")
        current = center_momentum * current + (1.0 - center_momentum) * sums / count
    return (jnp.stack(results), current)


def solution(mesh):
    placed = (
        P(None, ("dp", "head"), None, None),
        P(None, ("dp", "head"), None),
        P("dp", None),
        P("dp", None),
        P("dp", "head"),
        P(),
    )
    return jax.shard_map(
        shards,
        mesh=mesh,
        in_specs=placed,
        out_specs=(P(None, ("dp", "head"), None), P("head")),
        check_vma=False,
    )
```

profile of v0, /device:TPU:1, one launch (start us, length us, event | category | flops | bytes accessed | tf_op | source)
XLA Modules:
  0.0 333.8 jit_solution(7241315694982971049)
XLA Ops:
  7.2 0.7 all-gather.2.cloned.1.call-update
  7.9 1.9 broadcast_in_dim.124
  9.8 11.6 %all-to-all-start = ((bf16[64,32,256]{2,1,0:T(8,128)(2,1)}), bf16[64,32,256]{2,1,0:T(8,128)(2,1)S(1)}, u32[]{:S(2)}, u32[]{:S(2)}) async-start(bf16[64,32,256]{2,1,0:T(8,128)(2,1)} %broadcast_in_dim.124), calls=%async_computation | async-start | bytes 2097152 | tf_op jit(solution)/shard_map/all_to_all | solution.py:18
  22.1 1.9 scatter_custom_fusion.1
  24.9 1.9 scatter_custom_fusion
  27.0 0.8 slice_reduce_fusion.3
  28.0 1.2 compare_and_fusion
  29.3 1.1 fusion.59
  30.7 0.8 gather_fusion
  31.5 0.8 gather_fusion.1
  32.3 1.3 iota_compare_fusion
  34.0 17.4 %all-to-all-done = bf16[64,32,256]{2,1,0:T(8,128)(2,1)S(1)} async-done(((bf16[64,32,256]{2,1,0:T(8,128)(2,1)}), bf16[64,32,256]{2,1,0:T(8,128)(2,1)S(1)}, u32[]{:S(2)}, u32[]{:S(2)}) %all-to-all-start) | async-done | bytes 1048608 | tf_op jit(solution)/shard_map/all_to_all | solution.py:18
  51.4 0.9 broadcast_in_dim.126
  52.3 6.3 %all-to-all-start.2 = ((bf16[64,4,1024]{2,1,0:T(4,128)(2,1)}), bf16[64,4,1024]{2,1,0:T(4,128)(2,1)S(1)}, u32[]{:S(2)}, u32[]{:S(2)}) async-start(bf16[64,4,1024]{2,1,0:T(4,128)(2,1)} %broadcast_in_dim.126), calls=%async_computation.2 | async-start | bytes 1048576 | tf_op jit(solution)/shard_map/all_to_all | solution.py:18
  58.6 43.6 %all-gather.2.cloned.1.call-done = bf16[1024,2048]{1,0:T(8,128)(2,1)} async-done(((bf16[16,2048]{1,0:T(8,128)(2,1)}), bf16[1024,2048]{1,0:T(8,128)(2,1)}) %all-gather.2.cloned.1.call-update) | async-done | bytes 4194320 | tf_op jit(solution)/shard_map/all_gather | solution.py:62
  102.3 6.9 %multiply_reduce_fusion = (f32[196]{0:T(256)S(1)}, f32[196,256]{1,0:T(8,128)S(1)}) fusion(bf16[2048,256]{1,0:T(8,128)(2,1)S(1)} %bitcast.35, bf16[196,1024]{1,0:T(8,128)(2,1)S(1)} %reshape.215, bf16[1024,2048]{1,0:T(8,128)(2,1)} %all-gather.2.cloned.1.call-done), kind=kOutput, calls=%fused_computation.45 | convolution fusion | flops 1053796160 | bytes 5845776 | tf_op jit(solution)/shard_map/dot_general | solution.py:68
  109.3 0.8 broadcast_in_dim.125
  110.1 7.5 %all-to-all-start.1 = ((bf16[8,98,256]{2,1,0:T(8,128)(2,1)}), bf16[8,98,256]{2,1,0:T(8,128)(2,1)S(1)}, u32[]{:S(2)}, u32[]{:S(2)}) async-start(bf16[8,98,256]{2,1,0:T(8,128)(2,1)} %broadcast_in_dim.125), calls=%async_computation.1 | async-start | bytes 851968 | tf_op jit(solution)/shard_map/all_to_all | solution.py:18
  117.6 0.7 dynamic_slice.3
  118.9 0.9 convert_element_type.54
  119.8 13.7 %all-to-all-done.1 = bf16[8,98,256]{2,1,0:T(8,128)(2,1)S(1)} async-done(((bf16[8,98,256]{2,1,0:T(8,128)(2,1)}), bf16[8,98,256]{2,1,0:T(8,128)(2,1)S(1)}, u32[]{:S(2)}, u32[]{:S(2)}) %all-to-all-start.1) | async-done | bytes 401440 | tf_op jit(solution)/shard_map/all_to_all | solution.py:18
  133.5 0.8 broadcast_in_dim.129
  134.3 4.1 %all-to-all-start.5 = ((bf16[8,98,256]{2,1,0:T(8,128)(2,1)}), bf16[8,98,256]{2,1,0:T(8,128)(2,1)}, u32[]{:S(2)}, u32[]{:S(2)}) async-start(bf16[8,98,256]{2,1,0:T(8,128)(2,1)} %broadcast_in_dim.129), calls=%async_computation.5 | async-start | bytes 851968 | tf_op jit(solution)/shard_map/all_to_all | solution.py:18
  138.4 0.9 reshape.217
  139.3 1.9 compare_reduce_fusion.1
  141.1 0.6 convert_reduce_fusion.1
  141.7 0.7 fusion
  142.4 11.8 %all-to-all-done.5 = bf16[8,98,256]{2,1,0:T(8,128)(2,1)} async-done(((bf16[8,98,256]{2,1,0:T(8,128)(2,1)}), bf16[8,98,256]{2,1,0:T(8,128)(2,1)}, u32[]{:S(2)}, u32[]{:S(2)}) %all-to-all-start.5) | async-done | bytes 401440 | tf_op jit(solution)/shard_map/all_to_all | solution.py:18
  154.2 0.6 broadcast_in_dim.128
  154.9 3.3 all-to-all-start.3
  158.2 0.7 pad_maximum_fusion.2
  158.9 6.1 %all-to-all-done.3 = f32[8,1,784]{2,1,0:T(1,128)S(1)} async-done(((f32[8,1,784]{2,1,0:T(1,128)}), f32[8,1,784]{2,1,0:T(1,128)S(1)}, u32[]{:S(2)}, u32[]{:S(2)}) %all-to-all-start.3) | async-done | bytes 25120 | tf_op jit(solution)/shard_map/all_to_all | solution.py:18
  165.0 0.9 broadcast_in_dim.131
  165.8 7.9 %all-to-all-start.6 = ((f32[64,1,1025]{2,1,0:T(1,128)}), f32[64,1,1025]{2,1,0:T(1,128)S(1)}, u32[]{:S(2)}, u32[]{:S(2)}) async-start(f32[64,1,1025]{2,1,0:T(1,128)} %broadcast_in_dim.131), calls=%async_computation.6 | async-start | bytes 589824 | tf_op jit(solution)/shard_map/all_to_all | solution.py:18
  173.7 1.9 reshape.218
  175.6 10.7 %all-to-all-done.6 = f32[64,1,1025]{2,1,0:T(1,128)S(1)} async-done(((f32[64,1,1025]{2,1,0:T(1,128)}), f32[64,1,1025]{2,1,0:T(1,128)S(1)}, u32[]{:S(2)}, u32[]{:S(2)}) %all-to-all-start.6) | async-done | bytes 262432 | tf_op jit(solution)/shard_map/all_to_all | solution.py:18
  186.5 0.5 slice.81
  187.0 1.3 fusion.21
  188.4 2.1 fusion.58
  190.5 1.7 copy-done
  192.2 0.5 compare_reduce_fusion
  192.7 0.6 convert_reduce_fusion
  193.3 0.6 broadcast_in_dim.132
  193.9 3.3 all-to-all-start.7
  197.2 0.7 pad_maximum_fusion.3
  197.9 6.1 %all-to-all-done.7 = f32[8,1,784]{2,1,0:T(1,128)S(1)} async-done(((f32[8,1,784]{2,1,0:T(1,128)}), f32[8,1,784]{2,1,0:T(1,128)S(1)}, u32[]{:S(2)}, u32[]{:S(2)}) %all-to-all-start.7) | async-done | bytes 25120 | tf_op jit(solution)/shard_map/all_to_all | solution.py:18
  204.0 0.9 broadcast_in_dim.133
  204.8 7.2 %all-to-all-start.9 = ((f32[64,1,1025]{2,1,0:T(1,128)}), f32[64,1,1025]{2,1,0:T(1,128)S(1)}, u32[]{:S(2)}, u32[]{:S(2)}) async-start(f32[64,1,1025]{2,1,0:T(1,128)} %broadcast_in_dim.133), calls=%async_computation.9 | async-start | bytes 589824 | tf_op jit(solution)/shard_map/all_to_all | solution.py:18
  212.1 2.1 select_convert_fusion.1
  214.2 2.5 all_to_all.56
  216.7 8.0 %all-to-all-done.9 = f32[64,1,1025]{2,1,0:T(1,128)S(1)} async-done(((f32[64,1,1025]{2,1,0:T(1,128)}), f32[64,1,1025]{2,1,0:T(1,128)S(1)}, u32[]{:S(2)}, u32[]{:S(2)}) %all-to-all-start.9) | async-done | bytes 262432 | tf_op jit(solution)/shard_map/all_to_all | solution.py:18
  224.7 4.3 %all-to-all-start.4 = ((bf16[8,98,1024]{2,1,0:T(8,128)(2,1)}), bf16[8,98,1024]{2,1,0:T(8,128)(2,1)}, u32[]{:S(2)}, u32[]{:S(2)}) async-start(bf16[8,98,1024]{2,1,0:T(8,128)(2,1)} %all_to_all.56), calls=%async_computation.4 | async-start | bytes 3407872 | tf_op jit(solution)/shard_map/all_to_all | solution.py:90
  229.0 2.1 select_convert_fusion
  231.1 2.5 all_to_all.62
  233.7 36.0 %all-to-all-done.4 = bf16[8,98,1024]{2,1,0:T(8,128)(2,1)} async-done(((bf16[8,98,1024]{2,1,0:T(8,128)(2,1)}), bf16[8,98,1024]{2,1,0:T(8,128)(2,1)}, u32[]{:S(2)}, u32[]{:S(2)}) %all-to-all-start.4) | async-done | bytes 1605664 | tf_op jit(solution)/shard_map/all_to_all | solution.py:90
  269.7 3.9 %all-to-all-start.8 = ((bf16[8,98,1024]{2,1,0:T(8,128)(2,1)}), bf16[8,98,1024]{2,1,0:T(8,128)(2,1)S(1)}, u32[]{:S(2)}, u32[]{:S(2)}) async-start(bf16[8,98,1024]{2,1,0:T(8,128)(2,1)} %all_to_all.62), calls=%async_computation.8 | async-start | bytes 3407872 | tf_op jit(solution)/shard_map/all_to_all | solution.py:90
  273.8 0.5 slice.83
  274.4 1.2 fusion.19
  275.6 3.5 %copy.42 = bf16[98,8,1024]{2,1,0:T(8,128)(2,1)} copy(bf16[98,8,1024]{2,0,1:T(8,128)(2,1)} %bitcast.13) | data formatting | bytes 3211264 | tf_op jit(solution)/shard_map/all_to_all | solution.py:90
  279.1 2.7 stack.21
  281.8 35.1 %all-to-all-done.8 = bf16[8,98,1024]{2,1,0:T(8,128)(2,1)S(1)} async-done(((bf16[8,98,1024]{2,1,0:T(8,128)(2,1)}), bf16[8,98,1024]{2,1,0:T(8,128)(2,1)S(1)}, u32[]{:S(2)}, u32[]{:S(2)}) %all-to-all-start.8) | async-done | bytes 1605664 | tf_op jit(solution)/shard_map/all_to_all | solution.py:90
  316.9 2.0 copy.45
  318.9 2.7 stack.22
  321.9 5.0 %copy.47 = bf16[2,98,8192]{2,0,1:T(2,128)(2,1)} copy(bf16[2,98,8192]{2,1,0:T(8,128)(2,1)S(1)} %pad_maximum_fusion) | data formatting | bytes 6422528
  (51 shorter events, 4.1 us)
Async XLA Ops:
  7.2 14.3 %copy-start.4 = (s32[2,1,196]{2,1,0:T(1,128)S(1)}, s32[2,1,196]{2,1,0:T(1,128)}, u32[]{:S(2)}) copy-start(s32[2,1,196]{2,1,0:T(1,128)} %param.9) | copy-start | bytes 4708
  7.2 95.1 %all-gather.2.cloned.1.call-start = ((), (), s32[]{:S(2)}) async-start(), calls=%async_computation.10 | async-start | bytes 4259840 | tf_op jit(solution)/shard_map/all_gather | solution.py:62
  7.9 21.4 %copy-start.2 = (bf16[2,1,196,1024]{3,0,2,1:T(2,128)(2,1)S(1)}, bf16[2,1,196,1024]{3,0,2,1:T(2,128)(2,1)}, u32[]{:S(2)}) copy-start(bf16[2,1,196,1024]{3,0,2,1:T(2,128)(2,1)} %param.8) | copy-start | bytes 2408452
  9.8 41.6 %all-to-all-start = ((bf16[64,32,256]{2,1,0:T(8,128)(2,1)}), bf16[64,32,256]{2,1,0:T(8,128)(2,1)S(1)}, u32[]{:S(2)}, u32[]{:S(2)}) async-start(bf16[64,32,256]{2,1,0:T(8,128)(2,1)} %broadcast_in_dim.124), calls=%async_computation | async-start | bytes 2097152 | tf_op jit(solution)/shard_map/all_to_all | solution.py:18
  32.3 19.1 %copy-start.3 = (bf16[4,1024]{1,0:T(4,128)(2,1)S(1)}, bf16[4,1024]{1,0:T(4,128)(2,1)}, u32[]{:S(2)}) copy-start(bf16[4,1024]{1,0:T(4,128)(2,1)} %param.12) | copy-start | bytes 24580
  52.3 57.0 %all-to-all-start.2 = ((bf16[64,4,1024]{2,1,0:T(4,128)(2,1)}), bf16[64,4,1024]{2,1,0:T(4,128)(2,1)S(1)}, u32[]{:S(2)}, u32[]{:S(2)}) async-start(bf16[64,4,1024]{2,1,0:T(4,128)(2,1)} %broadcast_in_dim.126), calls=%async_computation.2 | async-start | bytes 1048576 | tf_op jit(solution)/shard_map/all_to_all | solution.py:18
  110.1 23.4 %all-to-all-start.1 = ((bf16[8,98,256]{2,1,0:T(8,128)(2,1)}), bf16[8,98,256]{2,1,0:T(8,128)(2,1)S(1)}, u32[]{:S(2)}, u32[]{:S(2)}) async-start(bf16[8,98,256]{2,1,0:T(8,128)(2,1)} %broadcast_in_dim.125), calls=%async_computation.1 | async-start | bytes 851968 | tf_op jit(solution)/shard_map/all_to_all | solution.py:18
  134.3 20.0 %all-to-all-start.5 = ((bf16[8,98,256]{2,1,0:T(8,128)(2,1)}), bf16[8,98,256]{2,1,0:T(8,128)(2,1)}, u32[]{:S(2)}, u32[]{:S(2)}) async-start(bf16[8,98,256]{2,1,0:T(8,128)(2,1)} %broadcast_in_dim.129), calls=%async_computation.5 | async-start | bytes 851968 | tf_op jit(solution)/shard_map/all_to_all | solution.py:18
  154.9 10.1 %all-to-all-start.3 = ((f32[8,1,784]{2,1,0:T(1,128)}), f32[8,1,784]{2,1,0:T(1,128)S(1)}, u32[]{:S(2)}, u32[]{:S(2)}) async-start(f32[8,1,784]{2,1,0:T(1,128)} %broadcast_in_dim.128), calls=%async_computation.3 | async-start | bytes 57344 | tf_op jit(solution)/shard_map/all_to_all | solution.py:18
  165.8 20.5 %all-to-all-start.6 = ((f32[64,1,1025]{2,1,0:T(1,128)}), f32[64,1,1025]{2,1,0:T(1,128)S(1)}, u32[]{:S(2)}, u32[]{:S(2)}) async-start(f32[64,1,1025]{2,1,0:T(1,128)} %broadcast_in_dim.131), calls=%async_computation.6 | async-start | bytes 589824 | tf_op jit(solution)/shard_map/all_to_all | solution.py:18
  190.5 1.7 copy-start
  193.9 10.1 %all-to-all-start.7 = ((f32[8,1,784]{2,1,0:T(1,128)}), f32[8,1,784]{2,1,0:T(1,128)S(1)}, u32[]{:S(2)}, u32[]{:S(2)}) async-start(f32[8,1,784]{2,1,0:T(1,128)} %broadcast_in_dim.132), calls=%async_computation.7 | async-start | bytes 57344 | tf_op jit(solution)/shard_map/all_to_all | solution.py:18
  204.8 19.9 %all-to-all-start.9 = ((f32[64,1,1025]{2,1,0:T(1,128)}), f32[64,1,1025]{2,1,0:T(1,128)S(1)}, u32[]{:S(2)}, u32[]{:S(2)}) async-start(f32[64,1,1025]{2,1,0:T(1,128)} %broadcast_in_dim.133), calls=%async_computation.9 | async-start | bytes 589824 | tf_op jit(solution)/shard_map/all_to_all | solution.py:18
  216.7 12.3 %copy-start.1 = (f32[784,1024]{1,0:T(8,128)S(1)}, f32[784,1024]{1,0:T(8,128)}, u32[]{:S(2)}) copy-start(f32[784,1024]{1,0:T(8,128)} %copy-done) | copy-start | bytes 9633796
  224.7 45.0 %all-to-all-start.4 = ((bf16[8,98,1024]{2,1,0:T(8,128)(2,1)}), bf16[8,98,1024]{2,1,0:T(8,128)(2,1)}, u32[]{:S(2)}, u32[]{:S(2)}) async-start(bf16[8,98,1024]{2,1,0:T(8,128)(2,1)} %all_to_all.56), calls=%async_computation.4 | async-start | bytes 3407872 | tf_op jit(solution)/shard_map/all_to_all | solution.py:90
  269.7 47.1 %all-to-all-start.8 = ((bf16[8,98,1024]{2,1,0:T(8,128)(2,1)}), bf16[8,98,1024]{2,1,0:T(8,128)(2,1)S(1)}, u32[]{:S(2)}, u32[]{:S(2)}) async-start(bf16[8,98,1024]{2,1,0:T(8,128)(2,1)} %all_to_all.62), calls=%async_computation.8 | async-start | bytes 3407872 | tf_op jit(solution)/shard_map/all_to_all | solution.py:90
Sparse Core Ops, SparseCore 0:
  11.3 90.8 all-gather.1
where the time goes:
time: 335 us; the launch traced here: 334 us
  waiting for transfers between devices  189 us (56%)
  starting transfers between devices  59.5 us (18%)
  local copies, waits for them, and re-layouts  39.1 us (12%)
  other arithmetic  20.7 us (6%)
  between operations  14.4 us (4%)
  matrix products  10.9 us (3%)
    all_to_all x8, waiting for transfers between devices, from_everyone(): lax.all_to_all(jnp.broadcast_to(x[None], (length, *x.shape)), axis, 0, 0,...  73.8 us
    all_to_all x2, waiting for transfers between devices, shards(): lax.all_to_all(shares, 'head', split_axis=0, concat_axis=1, tiled=True)  71.1 us
    all_to_all x8, starting transfers between devices, from_everyone(): lax.all_to_all(jnp.broadcast_to(x[None], (length, *x.shape)), axis, 0, 0,...  51.3 us
    all_gather x1, waiting for transfers between devices, shards(): piece = lax.all_gather(w_first, 'dp', axis=0, tiled=True)  43.6 us
    all_to_all x4, local copies, waits for them, and re-layouts, shards(): lax.all_to_all(shares, 'head', split_axis=0, concat_axis=1, tiled=True)  10.6 us
    all_to_all x2, starting transfers between devices, shards(): lax.all_to_all(shares, 'head', split_axis=0, concat_axis=1, tiled=True)  8.21 us
    broadcast_in_dim x8, local copies, waits for them, and re-layouts, from_everyone(): jnp.broadcast_to(x[None], (length, *x.shape))  7.34 us
    dot_general x1, matrix products, shards(): jnp.dot(part, collect(w_second, 'dp', 0), preferred_element_type=jnp.floa...  6.91 us
  transfers between devices with their start and end apart: 11, of which 10 were waited for; matrix products, arithmetic and copies ran while one was open for 13% of the time, Pallas kernels for 0%

commit v1 on v0

v1 whole, which is shorter than its diff:
```python
import functools

import jax
import jax.numpy as jnp
from jax import lax
from jax.experimental import pallas as pl
from jax.experimental.pallas import tpu as pltpu
from jax.sharding import PartitionSpec as P

MESH = pl.DeviceIdType.MESH
ANY = pl.BlockSpec(memory_space=pl.ANY)
VM = pl.BlockSpec(memory_space=pltpu.VMEM)

teacher_temp = 0.04
center_momentum = 0.9

NX, NY, NZ = 4, 8, 8
VIEWS, PATCH, CAP, PADCAP = 2, 196, 98, 104
D, HID, BOT, PROTO = 1024, 2048, 256, 8192
SHARE = PROTO // NZ
ACOLS = 1024
WCOLS = HID + 2 * BOT
F32 = jnp.float32
BF16 = jnp.bfloat16


def place():
    dp = lax.axis_index("dp")
    z = lax.axis_index("head")
    return dp // (2 * NY), (dp // 2) % NY, dp % 2, z


def dp_of(x, y, c):
    return (x * NY + y) * 2 + c


Y_ORDER = (0, 1, 7, 2, 6, 3, 5, 4)
RIGHT_HALF = (0, 7, 2, 5)


def plan():
    events = []
    for d, t in ((1, 2.6), (3, 2.7), (2, 3.3)):
        events.append((t, "ax", 0, d, 0))
    avail = {0: 0.0}
    for k in range(1, 5):
        for side in (0, 1):
            events.append((3.0 + 2.6 * (k - 1) + 0.01 * side, "by", side, k, 0))
            events.append((4.6 + 2.6 * (k - 1) + 0.01 * side, "py", side, k, 0))
        avail[k] = avail[8 - k] = 3.0 + 2.6 * (k - 1)
    pavail = {0: 2.2}
    for k in range(1, 5):
        pavail[k] = pavail[8 - k] = 4.6 + 2.6 * (k - 1)
    start = {0: 0.0, 1: 2.6, 3: 2.7, 2: 3.3}
    clock = 3.0
    for k in range(1, 5):
        for side in (0, 1):
            for i, j in enumerate((0, 1, 3, 2)):
                if k == 4 and (j in (0, 1)) != (side == 0):
                    continue
                t = max(start[j] + 2.4 * k, 3.4 + 3.0 * (k - 1) + 0.75 * i)
                events.append((t + 0.01 * side, "ay", side, k, j))
    for k in (1, 2):
        for side in (0, 1):
            for i, d in enumerate(Y_ORDER):
                if k == 2 and (d in RIGHT_HALF) != (side == 0):
                    continue
                if k == 1:
                    t = max(avail[d] + 2.2, 2.5 + 1.2 * i)
                else:
                    t = max(avail[d] + 4.4, 12.0 + 0.6 * i)
                events.append((t + 0.01 * side, "bx", side, k, d))
    for k in range(1, 5):
        for side in (0, 1):
            for i, d in enumerate(Y_ORDER):
                if k == 4 and (d in RIGHT_HALF) != (side == 0):
                    continue
                t = max(pavail[d] + 2.0 * k, 4.5 + 5.6 * (k - 1) + 0.7 * i)
                events.append((t + 0.01 * side, "pz", side, k, d))
    return sorted(events)


EVENTS = plan()


def gather_kernel(w1, w2, pw, wbuf, pbuf, px, lsem, px_s, px_r, ax_s, ax_r,
                  by_s, by_r, py_s, py_r, ay_s, ay_r, bx_s, bx_r, pz_s, pz_r, dd_s, dd_r):
    x, y, c, z = place()

    def at_x(n):
        return lax.rem(x + n + NX, NX)

    def at_y(n):
        return lax.rem(y + n + NY, NY)

    def at_z(n):
        return lax.rem(z + n + NZ, NZ)

    def dev(nx=0, ny=0, nz=0, other=False):
        return (dp_of(at_x(nx), at_y(ny), 1 - c if other else c), at_z(nz))

    cols_a, cols_b = pl.ds(0, ACOLS), pl.ds(ACOLS, WCOLS - ACOLS)
    loads = [
        pltpu.make_async_copy(pw, px.at[x], lsem.at[0]),
        pltpu.make_async_copy(w1, wbuf.at[x, y, c, :, pl.ds(0, HID)], lsem.at[1]),
        pltpu.make_async_copy(w2.at[pl.ds(0, 16)], wbuf.at[x, y, c, :, pl.ds(HID, BOT)], lsem.at[2]),
        pltpu.make_async_copy(w2.at[pl.ds(16, 16)], wbuf.at[x, y, c, :, pl.ds(HID + BOT, BOT)], lsem.at[3]),
    ]
    for copy in loads:
        copy.start()
    peers = [dev(nx=n) for n in (1, 2, 3)] + [dev(ny=1), dev(ny=-1), dev(nz=1), dev(nz=-1), dev(other=True)]
    barrier = pltpu.get_barrier_semaphore()
    for peer in peers:
        pl.semaphore_signal(barrier, inc=1, device_id=peer, device_id_type=MESH)
    pl.semaphore_wait(barrier, len(peers))
    for copy in loads:
        copy.wait()

    sent = []

    def send(ref, s, r, to):
        copy = pltpu.make_async_remote_copy(
            src_ref=ref, dst_ref=ref, send_sem=s, recv_sem=r, device_id=to, device_id_type=MESH
        )
        copy.start()
        sent.append(copy)

    def landed(ref, s, r, to):
        pltpu.make_async_remote_copy(
            src_ref=ref, dst_ref=ref, send_sem=s, recv_sem=r, device_id=to, device_id_type=MESH
        ).wait_recv()

    def half(cols, side):
        start, size = cols
        return pl.ds(start + side * (size // 2), size // 2)

    BALL, PALL = (ACOLS, WCOLS - ACOLS), (0, SHARE)

    def a_ref(nx, ny):
        return wbuf.at[at_x(nx), at_y(ny), c, :, cols_a]

    def b_ref(nx, ny, side=None):
        cols = cols_b if side is None else half(BALL, side)
        return wbuf.at[at_x(nx), at_y(ny), c, :, cols]

    def p_ref(nz, ny, side=None):
        cols = pl.ds(*PALL) if side is None else half(PALL, side)
        return pbuf.at[at_z(nz), c, at_y(ny), :, cols]

    def sgn(side):
        return 1 if side == 0 else -1

    def back(side, k):
        return -k * sgn(side)

    counts = {}
    for g in range(NY):
        counts["a", g] = 4
        counts["p", g] = 8
    for g in range(NX):
        counts["b", g] = 8
    counts["b", 0] = 9
    counts["p", 0] = 9
    counts["b", 2], counts["p", 4] = 8, 8

    def done(kind, g):
        counts[kind, g] -= 1
        if counts[kind, g]:
            return
        to = dev(other=True)
        if kind == "a":
            send(wbuf.at[:, at_y(-g), c, :, cols_a], dd_s.at[g], dd_r.at[g], to)
        elif kind == "b":
            send(wbuf.at[at_x(-g), :, c, :, cols_b], dd_s.at[8 + g], dd_r.at[8 + g], to)
        else:
            send(pbuf.at[at_z(-g), c], dd_s.at[12 + g], dd_r.at[12 + g], to)

    def forward_by(side, k):
        if k <= 3:
            send(b_ref(0, back(side, k - 1)), by_s.at[side, k - 1], by_r.at[side, k - 1], dev(ny=sgn(side)))
        else:
            send(b_ref(0, back(side, 3), side), by_s.at[side, 3], by_r.at[side, 3], dev(ny=sgn(side)))

    def forward_py(side, k):
        if k <= 3:
            send(p_ref(0, back(side, k - 1)), py_s.at[side, k - 1], py_r.at[side, k - 1], dev(ny=sgn(side)))
        else:
            send(p_ref(0, back(side, 3), side), py_s.at[side, 3], py_r.at[side, 3], dev(ny=sgn(side)))

    def forward_ay(side, k, j):
        if k == 4 and (j in (0, 1)) != (side == 0):
            return
        send(a_ref(-j, back(side, k - 1)), ay_s.at[side, k - 1, j], ay_r.at[side, k - 1, j], dev(ny=sgn(side)))

    def forward_bx(side, k, d):
        if k == 2 and (d in RIGHT_HALF) != (side == 0):
            return
        send(b_ref(back(side, k - 1), -d), bx_s.at[side, k - 1, d], bx_r.at[side, k - 1, d], dev(nx=sgn(side)))

    def forward_pz(side, k, d):
        if k == 4 and (d in RIGHT_HALF) != (side == 0):
            return
        send(p_ref(back(side, k - 1), -d), pz_s.at[side, k - 1, d], pz_r.at[side, k - 1, d], dev(nz=sgn(side)))

    for n in (1, 3, 2):
        send(px.at[x], px_s.at[n], px_r.at[n], dev(nx=n))
    for n in (1, 3, 2):
        send(a_ref(0, 0), ax_s.at[n], ax_r.at[n], dev(nx=n))
    for side in (0, 1):
        forward_by(side, 1)
    for side in (0, 1):
        forward_bx(side, 1, 0)
        forward_ay(side, 1, 0)
    done("a", 0)
    done("b", 0)

    for n in (1, 3, 2):
        landed(px.at[at_x(-n)], px_s.at[n], px_r.at[n], dev(nx=n))
    pbuf[z, c, y] = px[...].reshape(16, SHARE)
    early = [e for e in EVENTS if e[1] in ("ax", "by") and e[0] < 3.2]
    late = [e for e in EVENTS if e not in early]

    def handle(event):
        _, stream, side, k, j = event
        if stream == "ax":
            landed(a_ref(-k, 0), ax_s.at[k], ax_r.at[k], dev(nx=k))
            for s in (0, 1):
                forward_ay(s, 1, k)
            done("a", 0)
        elif stream == "by":
            ref = b_ref(0, back(side, k), None if k < 4 else side)
            landed(ref, by_s.at[side, k - 1], by_r.at[side, k - 1], dev(ny=1))
            if k < 4:
                forward_by(side, k + 1)
            counts["y4"] = counts.get("y4", 0) + (k == 4)
            if k < 4 or counts["y4"] == 2:
                for s in (0, 1):
                    forward_bx(s, 1, k if side == 0 else 8 - k) if k < 4 else forward_bx(s, 1, 4)
            done("b", 0)
        elif stream == "py":
            ref = p_ref(0, back(side, k), None if k < 4 else side)
            landed(ref, py_s.at[side, k - 1], py_r.at[side, k - 1], dev(ny=1))
            if k < 4:
                forward_py(side, k + 1)
            counts["p4"] = counts.get("p4", 0) + (k == 4)
            if k < 4 or counts["p4"] == 2:
                for s in (0, 1):
                    forward_pz(s, 1, k if side == 0 else 8 - k) if k < 4 else forward_pz(s, 1, 4)
            done("p", 0)
        elif stream == "ay":
            landed(a_ref(-j, back(side, k)), ay_s.at[side, k - 1, j], ay_r.at[side, k - 1, j], dev(ny=1))
            if k < 4:
                forward_ay(side, k + 1, j)
            done("a", k if side == 0 else 8 - k)
        elif stream == "bx":
            landed(b_ref(back(side, k), -j), bx_s.at[side, k - 1, j], bx_r.at[side, k - 1, j], dev(nx=1))
            if k < 2:
                forward_bx(side, k + 1, j)
            done("b", k if side == 0 else 4 - k)
        else:
            landed(p_ref(back(side, k), -j), pz_s.at[side, k - 1, j], pz_r.at[side, k - 1, j], dev(nz=1))
            if k < 4:
                forward_pz(side, k + 1, j)
            done("p", k if side == 0 else 8 - k)

    for event in early:
        handle(event)
    for side in (0, 1):
        forward_py(side, 1)
        forward_pz(side, 1, 0)
    done("p", 0)
    for event in late:
        handle(event)

    assert not any(v for k, v in counts.items() if isinstance(k, tuple)), counts
    other = 1 - c
    for g in range(8):
        landed(wbuf.at[:, at_y(-g), other, :, cols_a], dd_s.at[g], dd_r.at[g], dev(other=True))
        landed(pbuf.at[at_z(-g), other], dd_s.at[12 + g], dd_r.at[12 + g], dev(other=True))
    for g in range(4):
        landed(wbuf.at[at_x(-g), :, other, :, cols_b], dd_s.at[8 + g], dd_r.at[8 + g], dev(other=True))
    for copy in sent:
        copy.wait_send()


def gather(w_first, w_second, proto_weight):
    dma = pltpu.SemaphoreType.DMA
    return pl.pallas_call(
        gather_kernel,
        out_shape=(
            jax.ShapeDtypeStruct((NX, NY, 2, 16, WCOLS), BF16),
            jax.ShapeDtypeStruct((NZ, 2, NY, 16, SHARE), BF16),
        ),
        in_specs=[ANY] * 3,
        out_specs=(VM, VM),
        scratch_shapes=[
            pltpu.VMEM((NX, 4, SHARE), BF16),
            dma((4,)),
            dma((4,)), dma((4,)), dma((4,)), dma((4,)),
            dma((2, 4)), dma((2, 4)), dma((2, 4)), dma((2, 4)),
            dma((2, 4, 4)), dma((2, 4, 4)), dma((2, 2, 8)), dma((2, 2, 8)),
            dma((2, 4, 8)), dma((2, 4, 8)), dma((20,)), dma((20,)),
        ],
        compiler_params=pltpu.CompilerParams(
            collective_id=0, has_side_effects=True, vmem_limit_bytes=48 << 20
        ),
        name="gather",
    )(w_first, w_second, proto_weight)


def bottleneck_kernel(feats, mask, w, normed, sums, local, rows, hid):
    live = mask[...].astype(F32)
    counts = jnp.sum(live, axis=1, keepdims=True)
    before = lax.broadcasted_iota(jnp.int32, (PATCH, PATCH), 0) <= lax.broadcasted_iota(jnp.int32, (PATCH, PATCH), 1)
    live8 = jnp.concatenate([live, jnp.zeros((6, PATCH), F32)], axis=0)
    rank = jnp.dot(live8.astype(BF16), before.astype(BF16), preferred_element_type=F32)
    slot = lax.broadcasted_iota(jnp.int32, (PADCAP, PATCH), 0).astype(F32) + 1.0
    for v in range(VIEWS):
        pick = (rank[v : v + 1] == slot) & (live[v : v + 1] > 0.5)
        rows[pl.ds(v * PADCAP, PADCAP)] = jnp.dot(
            pick.astype(F32).astype(BF16), feats[v], preferred_element_type=F32
        ).astype(BF16)
    projected = jnp.zeros((VIEWS * PADCAP, BOT), F32)
    wide = HID // NX
    for t in range(NX):
        left = w[:, :, :, :, pl.ds(t * wide, wide)].reshape(D, wide)
        pre = jnp.dot(rows[...], left, preferred_element_type=F32)
        hidden = (0.5 * pre * (1.0 + lax.erf(pre * 0.5**0.5))).astype(BF16)
        low = w[t, :, :, :, pl.ds(HID, BOT)].reshape(16, 16, BOT)
        high = w[t, :, :, :, pl.ds(HID + BOT, BOT)].reshape(16, 16, BOT)
        right = jnp.stack([low, high], axis=1).reshape(wide, BOT)
        projected += jnp.dot(hidden, right, preferred_element_type=F32)
    scale = lax.rsqrt(jnp.sum(projected * projected, axis=-1, keepdims=True) + 1e-06)
    plain = (projected * scale).astype(BF16)
    to = lax.broadcasted_iota(jnp.int32, (BOT, BOT), 1)
    at = lax.broadcasted_iota(jnp.int32, (BOT, BOT), 0)
    source = ((to // 4) % NX) * 64 + ((to // 16) % NY) * 8 + (to // 128) * 4 + to % 4
    ordered = jnp.dot(plain, (at == source).astype(F32).astype(BF16), preferred_element_type=F32)
    normed[...] = ordered.astype(BF16)
    sums[...] = jnp.concatenate(
        [jnp.sum(ordered[v * PADCAP : (v + 1) * PADCAP], axis=0, keepdims=True) for v in range(VIEWS)]
        + [jnp.broadcast_to(counts, (VIEWS, BOT))],
        axis=0,
    )
    local[...] = jnp.broadcast_to(counts, (VIEWS, 128))


def bottleneck(features, patch_mask, w):
    return pl.pallas_call(
        bottleneck_kernel,
        out_shape=(
            jax.ShapeDtypeStruct((VIEWS * PADCAP, BOT), BF16),
            jax.ShapeDtypeStruct((2 * VIEWS, BOT), F32),
            jax.ShapeDtypeStruct((VIEWS, 128), F32),
        ),
        in_specs=[VM] * 3,
        out_specs=(VM,) * 3,
        scratch_shapes=[pltpu.VMEM((VIEWS * PADCAP, D), BF16), pltpu.VMEM((8, 128), F32)],
        compiler_params=pltpu.CompilerParams(vmem_limit_bytes=48 << 20),
        name="bottleneck",
    )(features, patch_mask, w)


def total_kernel(part, out, own, land, s_sem, r_sem):
    x, y, c, z = place()
    stages = (
        [(dp_of(x, y, c), lax.rem(z + n, NZ)) for n in range(1, 8)],
        [(dp_of(x, lax.rem(y + n, NY), c), z) for n in range(1, 8)],
        [(dp_of(lax.rem(x + n % 4, NX), y, lax.rem(c + n // 4, 2)), z) for n in range(1, 8)],
    )
    barrier = pltpu.get_barrier_semaphore()
    for stage in stages:
        for peer in stage:
            pl.semaphore_signal(barrier, inc=1, device_id=peer, device_id_type=MESH)
    pl.semaphore_wait(barrier, 21)
    own[0] = part[...]
    sent = []
    for i, stage in enumerate(stages):
        for n, peer in enumerate(stage):
            copy = pltpu.make_async_remote_copy(
                src_ref=own.at[i], dst_ref=land.at[i, n], send_sem=s_sem.at[i, n],
                recv_sem=r_sem.at[i, n], device_id=peer, device_id_type=MESH,
            )
            copy.start()
            sent.append(copy)
        total = own[i]
        for n in range(7):
            sent[i * 7 + n].wait_recv()
            total = total + land[i, n]
        if i < 2:
            own[i + 1] = total
        else:
            out[...] = total
    for copy in sent:
        copy.wait_send()


def total(part):
    return pl.pallas_call(
        total_kernel,
        out_shape=jax.ShapeDtypeStruct(part.shape, F32),
        in_specs=[VM],
        out_specs=VM,
        scratch_shapes=[
            pltpu.VMEM((3, *part.shape), F32),
            pltpu.VMEM((3, 7, *part.shape), F32),
            pltpu.SemaphoreType.DMA((3, 7)),
            pltpu.SemaphoreType.DMA((3, 7)),
        ],
        compiler_params=pltpu.CompilerParams(collective_id=1, has_side_effects=True),
        name="total",
    )(part)


def targets_kernel(normed, sums, local, protos, center, out, new_center, lhs, exps, totals):
    phase, j = pl.program_id(0), pl.program_id(1)
    z = lax.axis_index("head")
    rows = VIEWS * PADCAP

    @pl.when(phase == 0)
    def _():
        @pl.when(j == 0)
        def _():
            lhs[pl.ds(0, rows)] = normed[...]
            whole = sums[pl.ds(0, VIEWS)]
            high = whole.astype(BF16)
            rest = whole - high.astype(F32)
            mid = rest.astype(BF16)
            low = (rest - mid.astype(F32)).astype(BF16)
            lhs[pl.ds(rows, 16)] = jnp.concatenate(
                [high.astype(F32), mid.astype(F32), low.astype(F32), jnp.zeros((10, BOT), F32)], axis=0
            ).astype(BF16)
            totals[...] = jnp.zeros_like(totals)

        cols = pl.ds(pl.multiple_of(j * SHARE, SHARE), SHARE)
        block = protos[...].reshape(BOT, SHARE)
        wide = block.astype(F32)
        scale = lax.rsqrt(jnp.sum(wide * wide, axis=0, keepdims=True) + 1e-06)
        unit = (wide * scale).astype(BF16)
        logits = jnp.dot(lhs[...], unit, preferred_element_type=F32)
        current = center[...]
        for v in range(VIEWS):
            each = jnp.exp((logits[v * PADCAP : (v + 1) * PADCAP] - current) / teacher_temp)
            exps[pl.ds(v * PADCAP, PADCAP), cols] = each
            totals[pl.ds(v * PADCAP, PADCAP)] += jnp.broadcast_to(
                jnp.sum(each, axis=1, keepdims=True), (PADCAP, 128)
            )
            summed = logits[rows + v : rows + v + 1] + logits[rows + 2 + v : rows + 3 + v] + logits[rows + 4 + v : rows + 5 + v]
            count = sums[VIEWS + v, 0]
            current = center_momentum * current + (1.0 - center_momentum) * summed / count

        @pl.when(j == z)
        def _():
            new_center[...] = current

    @pl.when(phase == 1)
    def _():
        cols = pl.ds(pl.multiple_of(j * SHARE, SHARE), SHARE)
        slot = lax.broadcasted_iota(jnp.int32, (PADCAP, 1), 0).astype(F32)
        for v in range(VIEWS):
            every = totals[pl.ds(v * PADCAP, PADCAP), pl.ds(0, 1)]
            factor = jnp.where(slot < local[v, 0], PROTO / every, 0.0)
            probs = exps[pl.ds(v * PADCAP, PADCAP), cols] * factor
            out[v] = probs[:CAP].astype(BF16)


def targets_of(normed, sums, local, protos, center):
    full = lambda shape: pl.BlockSpec(shape, lambda p, j: (0,) * len(shape))
    last = NZ - 1
    return pl.pallas_call(
        targets_kernel,
        grid=(2, NZ),
        out_shape=(
            jax.ShapeDtypeStruct((VIEWS, CAP, PROTO), BF16),
            jax.ShapeDtypeStruct((1, SHARE), F32),
        ),
        in_specs=[
            full(normed.shape),
            full(sums.shape),
            full(local.shape),
            pl.BlockSpec((1, 2, NY, 16, SHARE), lambda p, j: (jnp.where(p == 0, j, last), 0, 0, 0, 0)),
            pl.BlockSpec((1, SHARE), lambda p, j: (0, jnp.where(p == 0, j, last))),
        ],
        out_specs=(
            pl.BlockSpec((VIEWS, CAP, SHARE), lambda p, j: (0, 0, p * j)),
            full((1, SHARE)),
        ),
        scratch_shapes=[
            pltpu.VMEM((VIEWS * PADCAP + 16, BOT), BF16),
            pltpu.VMEM((VIEWS * PADCAP, PROTO), F32),
            pltpu.VMEM((VIEWS * PADCAP, 128), F32),
        ],
        compiler_params=pltpu.CompilerParams(vmem_limit_bytes=48 << 20),
        name="targets",
    )(normed, sums, local, protos, center)


def shards(features, patch_mask, w_first, w_second, proto_weight, center):
    w, protos = gather(w_first, w_second, proto_weight)
    normed, part, local = bottleneck(features[:, 0], patch_mask[:, 0], w)
    sums = total(part)
    targets, new_center = targets_of(normed, sums, local, protos, center.reshape(1, PROTO))
    return targets, new_center.reshape(SHARE)


def solution(mesh):
    placed = (
        P(None, ("dp", "head"), None, None),
        P(None, ("dp", "head"), None),
        P("dp", None),
        P("dp", None),
        P("dp", "head"),
        P(),
    )
    return jax.shard_map(
        shards,
        mesh=mesh,
        in_specs=placed,
        out_specs=(P(None, ("dp", "head"), None), P("head")),
        check_vma=False,
    )
```

time: 335 us -> 105 us (0.31)
  waiting for transfers between devices: 189 us -> 0 us
  Pallas kernels: 0 us -> 88.1 us
  starting transfers between devices: 59.5 us -> 0 us
  local copies, waits for them, and re-layouts: 39.1 us -> 15.1 us
  other arithmetic: 20.7 us -> 0 us
  between operations: 14.4 us -> 0.72 us
  matrix products: 10.9 us -> 0 us
    all_to_all x10 -> x0, waiting for transfers between devices: 145 us -> none  [the longest x8 73.8 us: from_everyone(): lax.all_to_all(jnp.broadcast_to(x[None], (length, *x.shape)), axis, 0, 0,...]
    pallas_call x0 -> x4, Pallas kernels: none -> 88.1 us  [the longest x1 57.5 us: gather(): pl.pallas_call(gather_kernel, out_shape=(jax.ShapeDtypeStruct((NX, NY, 2,...]
    all_to_all x10 -> x0, starting transfers between devices: 59.5 us -> none  [the longest x8 51.3 us: from_everyone(): lax.all_to_all(jnp.broadcast_to(x[None], (length, *x.shape)), axis, 0, 0,...]
    all_gather x1 -> x0, waiting for transfers between devices: 43.6 us -> none  [shards(): piece = lax.all_gather(w_first, 'dp', axis=0, tiled=True)]
    dot_general x3 -> x0, matrix products: 10.9 us -> none  [the longest x1 6.91 us: shards(): jnp.dot(part, collect(w_second, 'dp', 0), preferred_element_type=jnp.floa...]
    all_to_all x4 -> x0, local copies, waits for them, and re-layouts: 10.6 us -> none  [shards(): lax.all_to_all(shares, 'head', split_axis=0, concat_axis=1, tiled=True)]
    unnamed x11 -> x19, local copies, waits for them, and re-layouts: 6.73 us -> 15.1 us
    broadcast_in_dim x8 -> x0, local copies, waits for them, and re-layouts: 7.34 us -> none  [from_everyone(): jnp.broadcast_to(x[None], (length, *x.shape))]
  transfers between devices with their start and end apart: 11 -> 0, of which waited for: 10 -> 0; matrix products, arithmetic and copies ran while one was open for 13% -> 0% of each run, Pallas kernels for 0% -> 0%
where the time goes in v1:
time: 105 us; the launch traced here: 104 us
  Pallas kernels  88.1 us (84%)
  local copies, waits for them, and re-layouts  15.1 us (14%)
    pallas_call x1, Pallas kernels, gather(): pl.pallas_call(gather_kernel, out_shape=(jax.ShapeDtypeStruct((NX, NY, 2,...  57.5 us
    pallas_call x1, Pallas kernels, total(): pl.pallas_call(total_kernel, out_shape=jax.ShapeDtypeStruct(part.shape, F...  19.4 us
    unnamed x19, local copies, waits for them, and re-layouts  15.1 us
    pallas_call x1, Pallas kernels, targets_of(): pl.pallas_call(targets_kernel, grid=(2, NZ), out_shape=(jax.ShapeDtypeStr...  9.31 us

profile of v1, /device:TPU:1, one launch (start us, length us, event | category | flops | bytes accessed | tf_op | source)
XLA Modules:
  0.0 103.9 jit_solution(1220054944333108595)
XLA Ops:
  0.6 0.0 copy-start.3
  0.6 0.7 copy.14
  1.3 1.3 %copy.13 = bf16[2,1,196,1024]{3,2,0,1:T(8,128)(2,1)S(1)} copy(bf16[2,1,196,1024]{3,0,2,1:T(2,128)(2,1)} %param.6) | data formatting | bytes 1605632 | tf_op args[0]
  2.7 0.0 copy-start.2
  2.7 0.8 copy-done.2
  3.5 0.0 copy-start.4
  3.5 0.7 copy-done.4
  4.2 0.0 copy-start.6
  4.2 0.7 copy-done.6
  4.9 57.5 %gather.1 = (bf16[4,8,2,16,2560]{4,3,2,1,0:T(8,128)(2,1)}, bf16[8,2,8,16,1024]{4,3,2,1,0:T(8,128)(2,1)S(1)}) custom-call(bf16[16,2048]{1,0:T(8,128)(2,1)S(1)} %copy-done.2, bf16[32,256]{1,0:T(8,128)(2,1)S(1)} %copy-done.4, bf16[4,1024]{1,0:T(4,128)(2,1)S(1)} %copy-done.6), custom_call_target="tpu_custom_call" | custom-call | tf_op jit(solution)/shard_map/gather/pallas_call | solution.py:288
  62.4 0.0 copy-start.1
  62.4 2.0 %copy-done.1 = bf16[8,2,8,16,1024]{4,3,2,1,0:T(8,128)(2,1)} copy-done((bf16[8,2,8,16,1024]{4,3,2,1,0:T(8,128)(2,1)}, bf16[8,2,8,16,1024]{4,3,2,1,0:T(8,128)(2,1)S(1)}, u32[]{:S(2)}) %copy-start.1) | copy-done | bytes 4194328
  64.4 0.0 copy-start
  64.4 2.5 %copy-done = bf16[4,8,2,16,2560]{4,3,2,1,0:T(8,128)(2,1)S(1)} copy-done((bf16[4,8,2,16,2560]{4,3,2,1,0:T(8,128)(2,1)S(1)}, bf16[4,8,2,16,2560]{4,3,2,1,0:T(8,128)(2,1)}, u32[]{:S(2)}) %copy-start) | copy-done | bytes 5242904
  66.9 1.9 %bottleneck.1 = (bf16[208,256]{1,0:T(8,128)(2,1)S(1)}, f32[4,256]{1,0:T(4,128)S(1)}, f32[2,128]{1,0:T(2,128)S(1)}) custom-call(bf16[2,196,1024]{2,1,0:T(8,128)(2,1)S(1)} %bitcast.8, s32[2,196]{1,0:T(2,128)S(1)} %bitcast.10, bf16[4,8,2,16,2560]{4,3,2,1,0:T(8,128)(2,1)S(1)} %copy-done), custom_call_target="tpu_custom_call" | custom-call | tf_op jit(solution)/shard_map/bottleneck/pallas_call | solution.py:349
  68.9 0.0 copy-start.7
  68.9 0.6 copy-done.7
  69.5 19.4 %total.1.sums = f32[4,256]{1,0:T(4,128)} custom-call(f32[4,256]{1,0:T(4,128)} %copy-done.7), custom_call_target="tpu_custom_call" | custom-call | tf_op jit(solution)/shard_map/total/pallas_call | solution.py:399
  88.9 0.0 copy-done.3
  88.9 0.0 copy-start.5
  88.9 0.7 copy-done.5
  89.6 9.3 %targets.1 = (bf16[2,98,8192]{2,1,0:T(8,128)(2,1)S(1)}, f32[1,1024]{1,0:T(1,128)}) custom-call(bf16[208,256]{1,0:T(8,128)(2,1)S(1)} %get-tuple-element.10.normed, f32[4,256]{1,0:T(4,128)S(1)} %copy-done.5, f32[2,128]{1,0:T(2,128)S(1)} %get-tuple-element.12.local, bf16[8,2,8,16,1024]{4,3,2,1,0:T(8,128)(2,1)} %copy-done.1, f32[1,8192]{1,0:T(1,128)S(1)} %bitcast.9), custom_call_target="tpu_custom_call" | custom-call | tf_op jit(solution)/shard_map/targets/pallas_call | solution.py:470
  98.9 5.0 %copy.9 = bf16[2,98,8192]{2,0,1:T(2,128)(2,1)} copy(bf16[2,98,8192]{2,1,0:T(8,128)(2,1)S(1)} %get-tuple-element.16) | data formatting | bytes 6422528
Async XLA Ops:
  0.6 88.3 %copy-start.3 = (f32[8192]{0:T(1024)S(1)}, f32[8192]{0:T(1024)}, u32[]{:S(2)}) copy-start(f32[8192]{0:T(1024)} %param.11) | copy-start | bytes 98308
  2.7 0.8 copy-start.2
  3.5 0.7 copy-start.4
  4.2 0.7 copy-start.6
  62.4 2.0 %copy-start.1 = (bf16[8,2,8,16,1024]{4,3,2,1,0:T(8,128)(2,1)}, bf16[8,2,8,16,1024]{4,3,2,1,0:T(8,128)(2,1)S(1)}, u32[]{:S(2)}) copy-start(bf16[8,2,8,16,1024]{4,3,2,1,0:T(8,128)(2,1)S(1)} %get-tuple-element.13.protos) | copy-start | bytes 12582916
  64.4 2.5 %copy-start = (bf16[4,8,2,16,2560]{4,3,2,1,0:T(8,128)(2,1)S(1)}, bf16[4,8,2,16,2560]{4,3,2,1,0:T(8,128)(2,1)}, u32[]{:S(2)}) copy-start(bf16[4,8,2,16,2560]{4,3,2,1,0:T(8,128)(2,1)} %get-tuple-element.9.w) | copy-start | bytes 15728644
  68.9 0.6 copy-start.7
  88.9 0.7 copy-start.5

commit v2 on v0

v2 whole, which is shorter than its diff:
```python
import functools

import jax
import jax.numpy as jnp
from jax import lax
from jax.experimental import pallas as pl
from jax.experimental.pallas import tpu as pltpu
from jax.sharding import PartitionSpec as P

MESH = pl.DeviceIdType.MESH
HBM = pl.BlockSpec(memory_space=pltpu.MemorySpace.HBM)
VM = pl.BlockSpec(memory_space=pltpu.VMEM)

teacher_temp = 0.04
center_momentum = 0.9

NX, NY, NZ = 4, 8, 8
VIEWS, PATCH, CAP, PADCAP = 2, 196, 98, 104
D, HID, BOT, PROTO = 1024, 2048, 256, 8192
SHARE = PROTO // NZ
ACOLS = 1024
WCOLS = HID + 2 * BOT
ROWS = VIEWS * PADCAP
VMEM_LIMIT = 36 << 20
F32 = jnp.float32
BF16 = jnp.bfloat16


def place():
    dp = lax.axis_index("dp")
    z = lax.axis_index("head")
    return dp // (2 * NY), (dp // 2) % NY, dp % 2, z


def dp_of(x, y, c):
    return (x * NY + y) * 2 + c


Y_ORDER = (0, 1, 7, 2, 6, 3, 5, 4)
RIGHT_HALF = (0, 7, 2, 5)
BY_TIME = {1: 4.2, 7: 4.3, 2: 5.8, 6: 5.9, 3: 7.8, 5: 7.9, 4: 9.8}
STEP = 3.8
MLP_AT = 26.0


def plan():
    events = []
    start = {0: 0.0, 1: 4.4, 3: 4.5, 2: 5.2}
    for d in (1, 3, 2):
        events.append((start[d], "ax", 0, d, 0))
    avail = {0: 0.0, **BY_TIME}
    for d, t in BY_TIME.items():
        events.append((t, "by", 0, d, 0))
    pavail = {0: 4.6}
    for k in range(1, 5):
        pavail[k] = pavail[8 - k] = 4.6 + 3.5 * k
        for side in (0, 1):
            events.append((pavail[k] + 0.01 * side, "py", side, k, 0))
    for k in range(1, 5):
        for side in (0, 1):
            for i, j in enumerate((0, 1, 3, 2)):
                if k == 4 and (j in (0, 1)) != (side == 0):
                    continue
                t = max(start[j] + STEP * k, 4.0 + STEP * (k - 1) + 0.75 * i)
                events.append((t + 0.01 * side, "ay", side, k, j))
    for k in (1, 2):
        for side in (0, 1):
            for i, d in enumerate(Y_ORDER):
                if k == 2 and (d in RIGHT_HALF) != (side == 0):
                    continue
                t = max(avail[d] + STEP, 3.0 + 1.2 * i)
                if k == 2:
                    t = max(t + STEP, 13.0 + 0.6 * i)
                events.append((t + 0.01 * side, "bx", side, k, d))
    whole = {0: pavail[4]}
    for k in range(1, 5):
        for side in (0, 1):
            for i, d in enumerate(Y_ORDER):
                if k == 4 and (d in RIGHT_HALF) != (side == 0):
                    continue
                t = max(pavail[d] + STEP * k, 8.0 + 5.7 * (k - 1) + 0.7 * i)
                events.append((t + 0.01 * side, "pz", side, k, d))
                g = k if side == 0 else 8 - k
                whole[g] = max(whole.get(g, 0.0), t + 0.01 * side)
    events.append((MLP_AT, "mlp", 0, 0, 0))
    sums = [MLP_AT + 2.0 + 5.0 * i for i in (1, 2, 3)]
    for i, t in enumerate(sums):
        events.append((t, "sum", i, 0, 0))
    ready = MLP_AT + 2.0
    for g in sorted(whole, key=whole.get):
        ready = max(ready + 0.7, whole[g] + 2.0)
        events.append((ready, "grp", 0, g, 0))
    return sorted(events)


EVENTS = plan()


def pick_rows(mask, fbuf, rows):
    live = jnp.concatenate([mask[0], mask[1], jnp.zeros((6, PATCH), jnp.int32)], axis=0).astype(F32)
    lanes = VIEWS * PATCH
    at = lax.broadcasted_iota(jnp.int32, (PATCH, lanes), 0)
    to = lax.broadcasted_iota(jnp.int32, (PATCH, lanes), 1)
    mixed = jnp.zeros((1, lanes), F32)
    for v in range(VIEWS):
        spread = (to == 2 * at + v).astype(F32).astype(BF16)
        mixed += jnp.dot(live.astype(BF16), spread, preferred_element_type=F32)[v : v + 1]
    at = lax.broadcasted_iota(jnp.int32, (lanes, lanes), 0)
    to = lax.broadcasted_iota(jnp.int32, (lanes, lanes), 1)
    before = ((at <= to) & ((to - at) % 2 == 0)).astype(F32).astype(BF16)
    mixed8 = jnp.broadcast_to(mixed, (8, lanes))
    rank = jnp.dot(mixed8.astype(BF16), before, preferred_element_type=F32)[0:1]
    row = lax.broadcasted_iota(jnp.int32, (ROWS, lanes), 0)
    lane = lax.broadcasted_iota(jnp.int32, (ROWS, lanes), 1)
    slot = (row // 2 + 1).astype(F32)
    same = (row - lane) % 2 == 0
    pick = ((rank == slot) & same & (mixed > 0.5)).astype(F32).astype(BF16)
    feats = fbuf[...].reshape(lanes, D)
    rows[...] = jnp.dot(pick, feats, preferred_element_type=F32).astype(BF16)
    return [jnp.sum(live[v : v + 1], axis=1, keepdims=True) for v in range(VIEWS)]


def bottleneck(rows, w, normed):
    projected = jnp.zeros((ROWS, BOT), F32)
    wide = HID // NX
    for t in range(NX):
        left = w[:, :, :, :, pl.ds(t * wide, wide)].reshape(D, wide)
        pre = jnp.dot(rows[...], left, preferred_element_type=F32)
        hidden = (0.5 * pre * (1.0 + lax.erf(pre * 0.5**0.5))).astype(BF16)
        low = w[t, :, :, :, pl.ds(HID, BOT)].reshape(16, 16, BOT)
        high = w[t, :, :, :, pl.ds(HID + BOT, BOT)].reshape(16, 16, BOT)
        right = jnp.stack([low, high], axis=1).reshape(wide, BOT)
        projected += jnp.dot(hidden, right, preferred_element_type=F32)
    scale = lax.rsqrt(jnp.sum(projected * projected, axis=-1, keepdims=True) + 1e-06)
    plain = (projected * scale).astype(BF16)
    to = lax.broadcasted_iota(jnp.int32, (BOT, BOT), 1)
    at = lax.broadcasted_iota(jnp.int32, (BOT, BOT), 0)
    source = ((to // 4) % NX) * 64 + ((to // 16) % NY) * 8 + (to // 128) * 4 + to % 4
    ordered = jnp.dot(plain, (at == source).astype(F32).astype(BF16), preferred_element_type=F32)
    normed[...] = ordered.astype(BF16)
    view = lax.broadcasted_iota(jnp.int32, (ROWS, BOT), 0) % 2
    return [jnp.sum(jnp.where(view == v, ordered, 0.0), axis=0, keepdims=True) for v in range(VIEWS)]


def main_kernel(feats, mask_in, w1, w2, pw, center_in, exps, weights, factors, new_center,
                wbuf, pbuf, ubuf, px, fbuf, mask, center, rows, normed, own, land, lsem,
                px_s, px_r, ax_s, ax_r, by_s, by_r, py_s, py_r, ay_s, ay_r, bx_s, bx_r,
                pz_s, pz_r, dd_s, dd_r, ar_s, ar_r):
    x, y, c, z = place()

    def at_x(n):
        return lax.rem(x + n + NX, NX)

    def at_y(n):
        return lax.rem(y + n + NY, NY)

    def at_z(n):
        return lax.rem(z + n + NZ, NZ)

    def dev(nx=0, ny=0, nz=0, other=False):
        return (dp_of(at_x(nx), at_y(ny), 1 - c if other else c), at_z(nz))

    rounds = (
        [dev(nz=n) for n in range(1, 8)],
        [dev(ny=n) for n in range(1, 8)],
        [dev(nx=n % 4, other=n >= 4) for n in range(1, 8)],
    )
    barrier = pltpu.get_barrier_semaphore()
    for peers in rounds:
        for peer in peers:
            pl.semaphore_signal(barrier, inc=1, device_id=peer, device_id_type=MESH)
    cols_a, cols_b = pl.ds(0, ACOLS), pl.ds(ACOLS, WCOLS - ACOLS)
    loads = [
        pltpu.make_async_copy(pw, px.at[x], lsem.at[0]),
        pltpu.make_async_copy(w1, wbuf.at[x, y, c, :, pl.ds(0, HID)], lsem.at[1]),
        pltpu.make_async_copy(w2.at[pl.ds(0, 16)], wbuf.at[x, y, c, :, pl.ds(HID, BOT)], lsem.at[2]),
        pltpu.make_async_copy(w2.at[pl.ds(16, 16)], wbuf.at[x, y, c, :, pl.ds(HID + BOT, BOT)], lsem.at[3]),
        pltpu.make_async_copy(feats, fbuf, lsem.at[4]),
        pltpu.make_async_copy(mask_in, mask, lsem.at[5]),
        pltpu.make_async_copy(center_in, center, lsem.at[6]),
    ]
    for copy in loads:
        copy.start()
    pl.semaphore_wait(barrier, 21)
    for copy in loads[:4]:
        copy.wait()

    sent = []

    def send(ref, s, r, to, dst=None):
        copy = pltpu.make_async_remote_copy(
            src_ref=ref, dst_ref=ref if dst is None else dst, send_sem=s, recv_sem=r, device_id=to, device_id_type=MESH
        )
        copy.start()
        sent.append(copy)

    def landed(ref, s, r, to):
        pltpu.make_async_remote_copy(
            src_ref=ref, dst_ref=ref, send_sem=s, recv_sem=r, device_id=to, device_id_type=MESH
        ).wait_recv()

    def a_ref(nx, ny):
        return wbuf.at[at_x(nx), at_y(ny), c, :, cols_a]

    def b_ref(nx, ny):
        return wbuf.at[at_x(nx), at_y(ny), c, :, cols_b]

    def p_ref(nz, ny, side=None):
        cols = pl.ds(0, SHARE) if side is None else pl.ds(side * (SHARE // 2), SHARE // 2)
        return pbuf.at[at_z(nz), c, at_y(ny), :, cols]

    def sgn(side):
        return 1 if side == 0 else -1

    def back(side, k):
        return -k * sgn(side)

    counts = {("p", 0): 9, ("p4"): 2}
    for g in range(NY):
        counts["a", g] = 4
        counts.setdefault(("p", g), 8)
    for g in range(NX):
        counts["b", g] = 8

    def done(kind, g):
        counts[kind, g] -= 1
        if counts[kind, g]:
            return
        to = dev(other=True)
        if kind == "a":
            send(wbuf.at[:, at_y(-g), c, :, cols_a], dd_s.at[g], dd_r.at[g], to)
        elif kind == "b":
            send(wbuf.at[at_x(-g), :, c, :, cols_b], dd_s.at[8 + g], dd_r.at[8 + g], to)
        else:
            send(pbuf.at[at_z(-g), c], dd_s.at[12 + g], dd_r.at[12 + g], to)

    def forward_py(side, k):
        ref = p_ref(0, back(side, k - 1), None if k <= 3 else side)
        send(ref, py_s.at[side, k - 1], py_r.at[side, k - 1], dev(ny=sgn(side)))

    def forward_ay(side, k, j):
        if k == 4 and (j in (0, 1)) != (side == 0):
            return
        send(a_ref(-j, back(side, k - 1)), ay_s.at[side, k - 1, j], ay_r.at[side, k - 1, j], dev(ny=sgn(side)))

    def forward_bx(side, k, d):
        if k == 2 and (d in RIGHT_HALF) != (side == 0):
            return
        send(b_ref(back(side, k - 1), -d), bx_s.at[side, k - 1, d], bx_r.at[side, k - 1, d], dev(nx=sgn(side)))

    def forward_pz(side, k, d):
        if k == 4 and (d in RIGHT_HALF) != (side == 0):
            return
        send(p_ref(back(side, k - 1), -d), pz_s.at[side, k - 1, d], pz_r.at[side, k - 1, d], dev(nz=sgn(side)))

    def sum_round(i):
        for n, peer in enumerate(rounds[i]):
            send(own.at[i], ar_s.at[i, n], ar_r.at[i, n], peer, land.at[i, n])

    for n in (1, 3, 2):
        send(px.at[x], px_s.at[n], px_r.at[n], dev(nx=n))
    for n in (1, 3, 2):
        send(a_ref(0, 0), ax_s.at[n], ax_r.at[n], dev(nx=n))
    for n in (1, 7, 2, 6, 3, 5, 4):
        send(b_ref(0, 0), by_s.at[n], by_r.at[n], dev(ny=n))
    for side in (0, 1):
        forward_bx(side, 1, 0)
        forward_ay(side, 1, 0)
    done("a", 0)
    done("b", 0)

    for copy in loads[4:]:
        copy.wait()
    local = pick_rows(mask, fbuf, rows)

    for n in (1, 3, 2):
        landed(px.at[at_x(-n)], px_s.at[n], px_r.at[n], dev(nx=n))
    pbuf[z, c, y] = px[...].reshape(16, SHARE)
    other = 1 - c

    def handle(event):
        _, kind, side, k, j = event
        if kind == "ax":
            landed(a_ref(-k, 0), ax_s.at[k], ax_r.at[k], dev(nx=k))
            for s in (0, 1):
                forward_ay(s, 1, k)
            done("a", 0)
        elif kind == "by":
            landed(b_ref(0, -k), by_s.at[k], by_r.at[k], dev(ny=k))
            for s in (0, 1):
                forward_bx(s, 1, k)
            done("b", 0)
        elif kind == "py":
            ref = p_ref(0, back(side, k), None if k < 4 else side)
            landed(ref, py_s.at[side, k - 1], py_r.at[side, k - 1], dev(ny=1))
            if k < 4:
                forward_py(side, k + 1)
            else:
                counts["p4"] -= 1
            if k < 4 or counts["p4"] == 0:
                for s in (0, 1):
                    forward_pz(s, 1, k if side == 0 else 8 - k)
            done("p", 0)
        elif kind == "ay":
            landed(a_ref(-j, back(side, k)), ay_s.at[side, k - 1, j], ay_r.at[side, k - 1, j], dev(ny=1))
            if k < 4:
                forward_ay(side, k + 1, j)
            done("a", k if side == 0 else 8 - k)
        elif kind == "bx":
            landed(b_ref(back(side, k), -j), bx_s.at[side, k - 1, j], bx_r.at[side, k - 1, j], dev(nx=1))
            if k < 2:
                forward_bx(side, k + 1, j)
            done("b", k if side == 0 else 4 - k)
        elif kind == "pz":
            landed(p_ref(back(side, k), -j), pz_s.at[side, k - 1, j], pz_r.at[side, k - 1, j], dev(nz=1))
            if k < 4:
                forward_pz(side, k + 1, j)
            done("p", k if side == 0 else 8 - k)
        elif kind == "mlp":
            for g in range(8):
                landed(wbuf.at[:, at_y(-g), other, :, cols_a], dd_s.at[g], dd_r.at[g], dev(other=True))
            for g in range(4):
                landed(wbuf.at[at_x(-g), :, other, :, cols_b], dd_s.at[8 + g], dd_r.at[8 + g], dev(other=True))
            sums = bottleneck(rows, wbuf, normed)
            own[0] = jnp.concatenate(sums + [jnp.broadcast_to(n, (1, BOT)) for n in local], axis=0)
            sum_round(0)
        elif kind == "sum":
            total = own[side]
            for n, peer in enumerate(rounds[side]):
                landed(land.at[side, n], ar_s.at[side, n], ar_r.at[side, n], peer)
                total = total + land[side, n]
            own[side + 1] = total
            if side < 2:
                sum_round(side + 1)
        else:
            at = at_z(-k)
            landed(pbuf.at[at, other], dd_s.at[12 + k], dd_r.at[12 + k], dev(other=True))
            wide = pbuf[at].reshape(BOT, SHARE).astype(F32)
            scale = lax.rsqrt(jnp.sum(wide * wide, axis=0, keepdims=True) + 1e-06)
            unit = (wide * scale).astype(BF16)
            ubuf[at] = unit
            logits = jnp.dot(normed[...], unit, preferred_element_type=F32)
            exps[:, pl.ds(pl.multiple_of(at * SHARE, SHARE), SHARE)] = jnp.exp(logits / teacher_temp)

    early = [e for e in EVENTS if e[1] in ("ax", "by") and e[0] < 4.55]
    for event in early:
        handle(event)
    for side in (0, 1):
        forward_py(side, 1)
        forward_pz(side, 1, 0)
    done("p", 0)
    for event in EVENTS:
        if event not in early:
            handle(event)
    assert not any(v for k, v in counts.items()), counts

    whole = own[3]
    high = whole[:VIEWS].astype(BF16).astype(F32)
    mid = (whole[:VIEWS] - high).astype(BF16).astype(F32)
    low = whole[:VIEWS] - high - mid
    parts = jnp.concatenate([high, mid, low, jnp.zeros((10, BOT), F32)], axis=0).astype(BF16)
    acc = jnp.zeros((ROWS, 128), F32)
    parity = lax.broadcasted_iota(jnp.int32, (8, SHARE), 0) % 2
    for at in range(NZ):
        cols = pl.ds(at * SHARE, SHARE)
        split = jnp.dot(parts, ubuf[at], preferred_element_type=F32)
        current, pair = center[:, cols], []
        for v in range(VIEWS):
            pair.append(jnp.exp(current / -teacher_temp))
            summed = split[v : v + 1] + split[2 + v : 3 + v] + split[4 + v : 5 + v]
            current = center_momentum * current + (1.0 - center_momentum) * summed / whole[VIEWS + v : VIEWS + v + 1, 0:1]
        pattern = jnp.where(parity == 0, pair[0], pair[1])
        weights[:, cols] = pattern
        shares = exps[:, cols].reshape(ROWS // 8, 8, SHARE) * pattern[None]
        shares = shares.reshape(ROWS, SHARE)
        for i in range(SHARE // 128):
            acc += shares[:, i * 128 : (i + 1) * 128]

        @pl.when(z == at)
        def _(current=current):
            new_center[...] = current

    row = lax.broadcasted_iota(jnp.int32, (ROWS, 1), 0)
    filled = jnp.where(row % 2 == 0, local[0], local[1]) > (row // 2).astype(F32)
    factor = jnp.where(filled, PROTO / jnp.sum(acc, axis=1, keepdims=True), 0.0)
    factors[...] = jnp.broadcast_to(factor, (ROWS, 128))
    for copy in sent:
        copy.wait_send()


def main_part(feats, patch_mask, w_first, w_second, proto_weight, center):
    dma = pltpu.SemaphoreType.DMA
    return pl.pallas_call(
        main_kernel,
        out_shape=(
            jax.ShapeDtypeStruct((ROWS, PROTO), F32),
            jax.ShapeDtypeStruct((8, PROTO), F32),
            jax.ShapeDtypeStruct((ROWS, 128), F32),
            jax.ShapeDtypeStruct((1, SHARE), F32),
        ),
        in_specs=[HBM] * 6,
        out_specs=(VM,) * 4,
        scratch_shapes=[
            pltpu.VMEM((NX, NY, 2, 16, WCOLS), BF16),
            pltpu.VMEM((NZ, 2, NY, 16, SHARE), BF16),
            pltpu.VMEM((NZ, BOT, SHARE), BF16),
            pltpu.VMEM((NX, 4, SHARE), BF16),
            pltpu.VMEM((PATCH, VIEWS, D), BF16),
            pltpu.VMEM((VIEWS, 1, PATCH), jnp.int32),
            pltpu.VMEM((1, PROTO), F32),
            pltpu.VMEM((ROWS, D), BF16),
            pltpu.VMEM((ROWS, BOT), BF16),
            pltpu.VMEM((4, 2 * VIEWS, BOT), F32),
            pltpu.VMEM((3, 7, 2 * VIEWS, BOT), F32),
            dma((7,)),
            dma((4,)), dma((4,)), dma((4,)), dma((4,)),
            dma((8,)), dma((8,)), dma((2, 4)), dma((2, 4)),
            dma((2, 4, 4)), dma((2, 4, 4)), dma((2, 2, 8)), dma((2, 2, 8)),
            dma((2, 4, 8)), dma((2, 4, 8)), dma((20,)), dma((20,)),
            dma((3, 7)), dma((3, 7)),
        ],
        compiler_params=pltpu.CompilerParams(
            collective_id=0, has_side_effects=True, vmem_limit_bytes=VMEM_LIMIT
        ),
        name="main_part",
    )(feats, patch_mask, w_first, w_second, proto_weight, center)


def write_kernel(exps, weights, factors, center, out, center_out):
    center_out[...] = center[...]
    for r in range(0, ROWS, 16):
        keep = min(16, VIEWS * CAP - r) // 2
        probs = []
        for h in (r, r + 8):
            probs.append(exps[pl.ds(h, 8)] * weights[...] * factors[pl.ds(h, 8), pl.ds(0, 1)])
        block = jnp.concatenate(probs, axis=0).astype(BF16)
        if keep > 0:
            out[pl.ds(r // 2, keep)] = block.reshape(8, VIEWS, block.shape[1])[:keep]


def write(exps, weights, factors, new_center):
    wide = 1024
    return pl.pallas_call(
        write_kernel,
        grid=(PROTO // wide,),
        out_shape=(
            jax.ShapeDtypeStruct((CAP, VIEWS, PROTO), BF16),
            jax.ShapeDtypeStruct((1, SHARE), F32),
        ),
        in_specs=[
            pl.BlockSpec((ROWS, wide), lambda j: (0, j)),
            pl.BlockSpec((8, wide), lambda j: (0, j)),
            pl.BlockSpec((ROWS, 128), lambda j: (0, 0)),
            pl.BlockSpec((1, SHARE), lambda j: (0, 0)),
        ],
        out_specs=(
            pl.BlockSpec((CAP, VIEWS, wide), lambda j: (0, 0, j)),
            pl.BlockSpec((1, SHARE), lambda j: (0, 0)),
        ),
        compiler_params=pltpu.CompilerParams(vmem_limit_bytes=16 << 20),
        name="write",
    )(exps, weights, factors, new_center)


def shards(features, patch_mask, w_first, w_second, proto_weight, center):
    feats = features[:, 0].transpose(1, 0, 2)
    inputs = (feats, patch_mask, w_first, w_second, proto_weight, center.reshape(1, PROTO))
    inputs = [pltpu.with_memory_space_constraint(a, pltpu.MemorySpace.HBM) for a in inputs]
    exps, weights, factors, new_center = main_part(*inputs)
    targets, new_center = write(exps, weights, factors, new_center)
    return targets.transpose(1, 0, 2), new_center.reshape(SHARE)


def solution(mesh):
    placed = (
        P(None, ("dp", "head"), None, None),
        P(None, ("dp", "head"), None),
        P("dp", None),
        P("dp", None),
        P("dp", "head"),
        P(),
    )
    return jax.shard_map(
        shards,
        mesh=mesh,
        in_specs=placed,
        out_specs=(P(None, ("dp", "head"), None), P("head")),
        check_vma=False,
    )
```

time: 335 us -> 75.6 us (0.23)
  waiting for transfers between devices: 189 us -> 0 us
  Pallas kernels: 0 us -> 74.9 us
  starting transfers between devices: 59.5 us -> 0 us
  local copies, waits for them, and re-layouts: 39.1 us -> 0 us
  other arithmetic: 20.7 us -> 0 us
  between operations: 14.4 us -> 0.64 us
  matrix products: 10.9 us -> 0 us
    all_to_all x10 -> x0, waiting for transfers between devices: 145 us -> none  [the longest x8 73.8 us: from_everyone(): lax.all_to_all(jnp.broadcast_to(x[None], (length, *x.shape)), axis, 0, 0,...]
    pallas_call x0 -> x2, Pallas kernels: none -> 74.9 us  [the longest x1 70.7 us: main_part(): pl.pallas_call(main_kernel, out_shape=(jax.ShapeDtypeStruct((ROWS, PROTO)...]
    all_to_all x10 -> x0, starting transfers between devices: 59.5 us -> none  [the longest x8 51.3 us: from_everyone(): lax.all_to_all(jnp.broadcast_to(x[None], (length, *x.shape)), axis, 0, 0,...]
    all_gather x1 -> x0, waiting for transfers between devices: 43.6 us -> none  [shards(): piece = lax.all_gather(w_first, 'dp', axis=0, tiled=True)]
    dot_general x3 -> x0, matrix products: 10.9 us -> none  [the longest x1 6.91 us: shards(): jnp.dot(part, collect(w_second, 'dp', 0), preferred_element_type=jnp.floa...]
    all_to_all x4 -> x0, local copies, waits for them, and re-layouts: 10.6 us -> none  [shards(): lax.all_to_all(shares, 'head', split_axis=0, concat_axis=1, tiled=True)]
    broadcast_in_dim x8 -> x0, local copies, waits for them, and re-layouts: 7.34 us -> none  [from_everyone(): jnp.broadcast_to(x[None], (length, *x.shape))]
    unnamed x11 -> x0, local copies, waits for them, and re-layouts: 6.73 us -> none
  transfers between devices with their start and end apart: 11 -> 0, of which waited for: 10 -> 0; matrix products, arithmetic and copies ran while one was open for 13% -> 0% of each run, Pallas kernels for 0% -> 0%
where the time goes in v2:
time: 75.6 us; the launch traced here: 75.5 us
  Pallas kernels  74.9 us (99%)
    pallas_call x1, Pallas kernels, main_part(): pl.pallas_call(main_kernel, out_shape=(jax.ShapeDtypeStruct((ROWS, PROTO)...  70.7 us
    pallas_call x1, Pallas kernels, write(): pl.pallas_call(write_kernel, grid=(PROTO // wide,), out_shape=(jax.ShapeD...  4.19 us

profile of v2, /device:TPU:1, one launch (start us, length us, event | category | flops | bytes accessed | tf_op | source)
XLA Modules:
  0.0 75.5 jit_solution(12725049106180033753)
XLA Ops:
  0.6 70.7 %main_part.1 = (f32[208,8192]{1,0:T(8,128)S(1)}, f32[8,8192]{1,0:T(8,128)S(1)}, f32[208,128]{1,0:T(8,128)S(1)}, f32[1,1024]{1,0:T(1,128)S(1)}) custom-call(bf16[196,2,1024]{2,1,0:T(2,128)(2,1)} %bitcast.6, s32[2,1,196]{2,1,0:T(1,128)} %mask_in.1, bf16[16,2048]{1,0:T(8,128)(2,1)} %w1.1, bf16[32,256]{1,0:T(8,128)(2,1)} %w2.1, bf16[4,1024]{1,0:T(4,128)(2,1)} %pw.1, ...), custom_call_target="tpu_custom_call" | custom-call | tf_op jit(solution)/shard_map/main_part/pallas_call | solution.py:393
  71.3 4.2 %write.1 = (bf16[98,2,8192]{2,1,0:T(2,128)(2,1)}, f32[1,1024]{1,0:T(1,128)}) custom-call(f32[208,8192]{1,0:T(8,128)S(1)} %get-tuple-element.8.exps, f32[8,8192]{1,0:T(8,128)S(1)} %get-tuple-element.9.weights, f32[208,128]{1,0:T(8,128)S(1)} %get-tuple-element.10.factors, f32[1,1024]{1,0:T(1,128)S(1)} %get-tuple-element.11.center), custom_call_target="tpu_custom_call" | custom-call | tf_op jit(solution)/shard_map/write/pallas_call | solution.py:443

commit v3 on v2

--- a/solution.py
+++ b/solution.py
@@ -38,9 +38,10 @@
 
 Y_ORDER = (0, 1, 7, 2, 6, 3, 5, 4)
 RIGHT_HALF = (0, 7, 2, 5)
-BY_TIME = {1: 4.2, 7: 4.3, 2: 5.8, 6: 5.9, 3: 7.8, 5: 7.9, 4: 9.8}
+BY_TIME = {1: 4.2, 7: 4.3, 2: 5.5, 6: 5.6, 3: 9.5, 5: 9.6, 4: 10.5}
+PX_TIME = {0: 6.5, 1: 11.5, 3: 11.6, 2: 12.6}
 STEP = 3.8
-MLP_AT = 26.0
+MLP_AT = 24.0
 
 
 def plan():
@@ -51,11 +52,10 @@
     avail = {0: 0.0, **BY_TIME}
     for d, t in BY_TIME.items():
         events.append((t, "by", 0, d, 0))
-    pavail = {0: 4.6}
-    for k in range(1, 5):
-        pavail[k] = pavail[8 - k] = 4.6 + 3.5 * k
-        for side in (0, 1):
-            events.append((pavail[k] + 0.01 * side, "py", side, k, 0))
+    events.append((BY_TIME[4] + 0.1, "by", 1, 4, 0))
+    events.append((PX_TIME[0], "pack", 0, 0, 0))
+    for d in (1, 3, 2):
+        events.append((PX_TIME[d], "px", 0, d, 0))
     for k in range(1, 5):
         for side in (0, 1):
             for i, j in enumerate((0, 1, 3, 2)):
@@ -72,20 +72,20 @@
                 if k == 2:
                     t = max(t + STEP, 13.0 + 0.6 * i)
                 events.append((t + 0.01 * side, "bx", side, k, d))
-    whole = {0: pavail[4]}
+    whole = {0: PX_TIME[2]}
     for k in range(1, 5):
         for side in (0, 1):
-            for i, d in enumerate(Y_ORDER):
-                if k == 4 and (d in RIGHT_HALF) != (side == 0):
-                    continue
-                t = max(pavail[d] + STEP * k, 8.0 + 5.7 * (k - 1) + 0.7 * i)
-                events.append((t + 0.01 * side, "pz", side, k, d))
-                g = k if side == 0 else 8 - k
-                whole[g] = max(whole.get(g, 0.0), t + 0.01 * side)
+            for i, d in enumerate((0, 1, 3, 2)):
+                for h in (0, 1):
+                    if k == 4 and h != side:
+                        continue
+                    t = max(PX_TIME[d] + STEP * k + 0.7 * h, 8.5 + 5.7 * (k - 1) + 1.4 * i + 0.7 * h)
+                    events.append((t + 0.01 * side, "pz", side, k, 2 * d + h))
+                    g = k if side == 0 else 8 - k
+                    whole[g] = max(whole.get(g, 0.0), t + 0.01 * side)
     events.append((MLP_AT, "mlp", 0, 0, 0))
-    sums = [MLP_AT + 2.0 + 5.0 * i for i in (1, 2, 3)]
-    for i, t in enumerate(sums):
-        events.append((t, "sum", i, 0, 0))
+    for i in range(3):
+        events.append((MLP_AT + 2.0 + 4.5 * (i + 1), "sum", i, 0, 0))
     ready = MLP_AT + 2.0
     for g in sorted(whole, key=whole.get):
         ready = max(ready + 0.7, whole[g] + 2.0)
@@ -135,7 +135,7 @@
     plain = (projected * scale).astype(BF16)
     to = lax.broadcasted_iota(jnp.int32, (BOT, BOT), 1)
     at = lax.broadcasted_iota(jnp.int32, (BOT, BOT), 0)
-    source = ((to // 4) % NX) * 64 + ((to // 16) % NY) * 8 + (to // 128) * 4 + to % 4
+    source = ((to // 32) % NX) * 64 + ((to // 4) % NY) * 8 + (to // 128) * 4 + to % 4
     ordered = jnp.dot(plain, (at == source).astype(F32).astype(BF16), preferred_element_type=F32)
     normed[...] = ordered.astype(BF16)
     view = lax.broadcasted_iota(jnp.int32, (ROWS, BOT), 0) % 2
@@ -143,7 +143,7 @@
 
 
 def main_kernel(feats, mask_in, w1, w2, pw, center_in, exps, weights, factors, new_center,
-                wbuf, pbuf, ubuf, px, fbuf, mask, center, rows, normed, own, land, lsem,
+                wbuf, pbuf, ubuf, stage, fbuf, mask, center, rows, normed, own, land, lsem,
                 px_s, px_r, ax_s, ax_r, by_s, by_r, py_s, py_r, ay_s, ay_r, bx_s, bx_r,
                 pz_s, pz_r, dd_s, dd_r, ar_s, ar_r):
     x, y, c, z = place()
@@ -171,7 +171,7 @@
             pl.semaphore_signal(barrier, inc=1, device_id=peer, device_id_type=MESH)
     cols_a, cols_b = pl.ds(0, ACOLS), pl.ds(ACOLS, WCOLS - ACOLS)
     loads = [
-        pltpu.make_async_copy(pw, px.at[x], lsem.at[0]),
+        pltpu.make_async_copy(pw, stage.at[y], lsem.at[0]),
         pltpu.make_async_copy(w1, wbuf.at[x, y, c, :, pl.ds(0, HID)], lsem.at[1]),
         pltpu.make_async_copy(w2.at[pl.ds(0, 16)], wbuf.at[x, y, c, :, pl.ds(HID, BOT)], lsem.at[2]),
         pltpu.make_async_copy(w2.at[pl.ds(16, 16)], wbuf.at[x, y, c, :, pl.ds(HID + BOT, BOT)], lsem.at[3]),
@@ -202,12 +202,14 @@
     def a_ref(nx, ny):
         return wbuf.at[at_x(nx), at_y(ny), c, :, cols_a]
 
-    def b_ref(nx, ny):
-        return wbuf.at[at_x(nx), at_y(ny), c, :, cols_b]
-
-    def p_ref(nz, ny, side=None):
-        cols = pl.ds(0, SHARE) if side is None else pl.ds(side * (SHARE // 2), SHARE // 2)
-        return pbuf.at[at_z(nz), c, at_y(ny), :, cols]
+    def b_ref(nx, ny, side=None):
+        wide = WCOLS - ACOLS
+        cols = cols_b if side is None else pl.ds(ACOLS + side * (wide // 2), wide // 2)
+        return wbuf.at[at_x(nx), at_y(ny), c, :, cols]
+
+    def p_ref(nz, nx, half=None):
+        part = pl.ds(0, 4 * NY) if half is None else pl.ds(half * 2 * NY, 2 * NY)
+        return pbuf.at[at_z(nz), c, at_x(nx), part]
 
     def sgn(side):
         return 1 if side == 0 else -1
@@ -215,12 +217,12 @@
     def back(side, k):
         return -k * sgn(side)
 
-    counts = {("p", 0): 9, ("p4"): 2}
+    counts = {("p", 0): 4, ("b", 0): 9, "far": 2}
     for g in range(NY):
         counts["a", g] = 4
         counts.setdefault(("p", g), 8)
     for g in range(NX):
-        counts["b", g] = 8
+        counts.setdefault(("b", g), 8)
 
     def done(kind, g):
         counts[kind, g] -= 1
@@ -234,10 +236,6 @@
         else:
             send(pbuf.at[at_z(-g), c], dd_s.at[12 + g], dd_r.at[12 + g], to)
 
-    def forward_py(side, k):
-        ref = p_ref(0, back(side, k - 1), None if k <= 3 else side)
-        send(ref, py_s.at[side, k - 1], py_r.at[side, k - 1], dev(ny=sgn(side)))
-
     def forward_ay(side, k, j):
         if k == 4 and (j in (0, 1)) != (side == 0):
             return
@@ -248,20 +246,20 @@
             return
         send(b_ref(back(side, k - 1), -d), bx_s.at[side, k - 1, d], bx_r.at[side, k - 1, d], dev(nx=sgn(side)))
 
-    def forward_pz(side, k, d):
-        if k == 4 and (d in RIGHT_HALF) != (side == 0):
+    def forward_pz(side, k, j):
+        if k == 4 and j % 2 != side:
             return
-        send(p_ref(back(side, k - 1), -d), pz_s.at[side, k - 1, d], pz_r.at[side, k - 1, d], dev(nz=sgn(side)))
+        send(p_ref(back(side, k - 1), -(j // 2), j % 2), pz_s.at[side, k - 1, j], pz_r.at[side, k - 1, j], dev(nz=sgn(side)))
 
     def sum_round(i):
         for n, peer in enumerate(rounds[i]):
             send(own.at[i], ar_s.at[i, n], ar_r.at[i, n], peer, land.at[i, n])
 
-    for n in (1, 3, 2):
-        send(px.at[x], px_s.at[n], px_r.at[n], dev(nx=n))
+    for n in (4, 3, 5, 2, 6, 1, 7):
+        send(stage.at[y], py_s.at[n], py_r.at[n], dev(ny=n))
     for n in (1, 3, 2):
         send(a_ref(0, 0), ax_s.at[n], ax_r.at[n], dev(nx=n))
-    for n in (1, 7, 2, 6, 3, 5, 4):
+    for n in (1, 7, 2, 6):
         send(b_ref(0, 0), by_s.at[n], by_r.at[n], dev(ny=n))
     for side in (0, 1):
         forward_bx(side, 1, 0)
@@ -273,9 +271,6 @@
         copy.wait()
     local = pick_rows(mask, fbuf, rows)
 
-    for n in (1, 3, 2):
-        landed(px.at[at_x(-n)], px_s.at[n], px_r.at[n], dev(nx=n))
-    pbuf[z, c, y] = px[...].reshape(16, SHARE)
     other = 1 - c
 
     def handle(event):
@@ -286,20 +281,34 @@
                 forward_ay(s, 1, k)
             done("a", 0)
         elif kind == "by":
-            landed(b_ref(0, -k), by_s.at[k], by_r.at[k], dev(ny=k))
-            for s in (0, 1):
-                forward_bx(s, 1, k)
+            slot = 8 if side else k
+            landed(b_ref(0, -k, side if k == 4 else None), by_s.at[slot], by_r.at[slot], dev(ny=k))
+            if k in (2, 6):
+                way = 1 if k == 2 else -1
+                near, far, half = (3, 4, 0) if k == 2 else (5, 8, 1)
+                send(b_ref(0, -k), by_s.at[near], by_r.at[near], dev(ny=way))
+                send(b_ref(0, -k, half), by_s.at[far], by_r.at[far], dev(ny=2 * way))
+            if k == 4:
+                counts["far"] -= 1
+            if k != 4 or counts["far"] == 0:
+                for s in (0, 1):
+                    forward_bx(s, 1, k)
             done("b", 0)
-        elif kind == "py":
-            ref = p_ref(0, back(side, k), None if k < 4 else side)
-            landed(ref, py_s.at[side, k - 1], py_r.at[side, k - 1], dev(ny=1))
-            if k < 4:
-                forward_py(side, k + 1)
-            else:
-                counts["p4"] -= 1
-            if k < 4 or counts["p4"] == 0:
+        elif kind == "pack":
+            for n in range(1, NY):
+                landed(stage.at[at_y(-n)], py_s.at[n], py_r.at[n], dev(ny=n))
+            pbuf[z, c, x] = stage[...].reshape(4 * NY, SHARE)
+            for n in (1, 3, 2):
+                send(p_ref(0, 0), px_s.at[n], px_r.at[n], dev(nx=n))
+            for j in (0, 1):
                 for s in (0, 1):
-                    forward_pz(s, 1, k if side == 0 else 8 - k)
+                    forward_pz(s, 1, j)
+            done("p", 0)
+        elif kind == "px":
+            landed(p_ref(0, -k), px_s.at[k], px_r.at[k], dev(nx=k))
+            for j in (2 * k, 2 * k + 1):
+                for s in (0, 1):
+                    forward_pz(s, 1, j)
             done("p", 0)
         elif kind == "ay":
             landed(a_ref(-j, back(side, k)), ay_s.at[side, k - 1, j], ay_r.at[side, k - 1, j], dev(ny=1))
@@ -312,7 +321,7 @@
                 forward_bx(side, k + 1, j)
             done("b", k if side == 0 else 4 - k)
         elif kind == "pz":
-            landed(p_ref(back(side, k), -j), pz_s.at[side, k - 1, j], pz_r.at[side, k - 1, j], dev(nz=1))
+            landed(p_ref(back(side, k), -(j // 2), j % 2), pz_s.at[side, k - 1, j], pz_r.at[side, k - 1, j], dev(nz=1))
             if k < 4:
                 forward_pz(side, k + 1, j)
             done("p", k if side == 0 else 8 - k)
@@ -342,16 +351,8 @@
             logits = jnp.dot(normed[...], unit, preferred_element_type=F32)
             exps[:, pl.ds(pl.multiple_of(at * SHARE, SHARE), SHARE)] = jnp.exp(logits / teacher_temp)
 
-    early = [e for e in EVENTS if e[1] in ("ax", "by") and e[0] < 4.55]
-    for event in early:
+    for event in EVENTS:
         handle(event)
-    for side in (0, 1):
-        forward_py(side, 1)
-        forward_pz(side, 1, 0)
-    done("p", 0)
-    for event in EVENTS:
-        if event not in early:
-            handle(event)
     assert not any(v for k, v in counts.items()), counts
 
     whole = own[3]
@@ -402,9 +403,9 @@
         out_specs=(VM,) * 4,
         scratch_shapes=[
             pltpu.VMEM((NX, NY, 2, 16, WCOLS), BF16),
-            pltpu.VMEM((NZ, 2, NY, 16, SHARE), BF16),
+            pltpu.VMEM((NZ, 2, NX, 4 * NY, SHARE), BF16),
             pltpu.VMEM((NZ, BOT, SHARE), BF16),
-            pltpu.VMEM((NX, 4, SHARE), BF16),
+            pltpu.VMEM((NY, 4, SHARE), BF16),
             pltpu.VMEM((PATCH, VIEWS, D), BF16),
             pltpu.VMEM((VIEWS, 1, PATCH), jnp.int32),
             pltpu.VMEM((1, PROTO), F32),
@@ -414,7 +415,7 @@
             pltpu.VMEM((3, 7, 2 * VIEWS, BOT), F32),
             dma((7,)),
             dma((4,)), dma((4,)), dma((4,)), dma((4,)),
-            dma((8,)), dma((8,)), dma((2, 4)), dma((2, 4)),
+            dma((9,)), dma((9,)), dma((8,)), dma((8,)),
             dma((2, 4, 4)), dma((2, 4, 4)), dma((2, 2, 8)), dma((2, 2, 8)),
             dma((2, 4, 8)), dma((2, 4, 8)), dma((20,)), dma((20,)),
             dma((3, 7)), dma((3, 7)),

time: 75.6 us -> 72.8 us (0.963)
  Pallas kernels: 74.9 us -> 72 us
    pallas_call x1, Pallas kernels: 70.7 us -> 67.8 us  [main_part(): pl.pallas_call(main_kernel, out_shape=(jax.ShapeDtypeStruct((ROWS, PROTO)...]
where the time goes in v3:
time: 72.8 us; the launch traced here: 72.7 us
  Pallas kernels  72 us (99%)
    pallas_call x1, Pallas kernels, main_part(): pl.pallas_call(main_kernel, out_shape=(jax.ShapeDtypeStruct((ROWS, PROTO)...  67.8 us
    pallas_call x1, Pallas kernels, write(): pl.pallas_call(write_kernel, grid=(PROTO // wide,), out_shape=(jax.ShapeD...  4.19 us

profile of v3, /device:TPU:1, one launch (start us, length us, event | category | flops | bytes accessed | tf_op | source)
XLA Modules:
  0.0 72.7 jit_solution(7044197742069303740)
XLA Ops:
  0.6 67.8 %main_part.1 = (f32[208,8192]{1,0:T(8,128)S(1)}, f32[8,8192]{1,0:T(8,128)S(1)}, f32[208,128]{1,0:T(8,128)S(1)}, f32[1,1024]{1,0:T(1,128)S(1)}) custom-call(bf16[196,2,1024]{2,1,0:T(2,128)(2,1)} %bitcast.6, s32[2,1,196]{2,1,0:T(1,128)} %mask_in.1, bf16[16,2048]{1,0:T(8,128)(2,1)} %w1.1, bf16[32,256]{1,0:T(8,128)(2,1)} %w2.1, bf16[4,1024]{1,0:T(4,128)(2,1)} %pw.1, ...), custom_call_target="tpu_custom_call" | custom-call | tf_op jit(solution)/shard_map/main_part/pallas_call | solution.py:394
  68.5 4.2 %write.1 = (bf16[98,2,8192]{2,1,0:T(2,128)(2,1)}, f32[1,1024]{1,0:T(1,128)}) custom-call(f32[208,8192]{1,0:T(8,128)S(1)} %get-tuple-element.8.exps, f32[8,8192]{1,0:T(8,128)S(1)} %get-tuple-element.9.weights, f32[208,128]{1,0:T(8,128)S(1)} %get-tuple-element.10.factors, f32[1,1024]{1,0:T(1,128)S(1)} %get-tuple-element.11.center), custom_call_target="tpu_custom_call" | custom-call | tf_op jit(solution)/shard_map/write/pallas_call | solution.py:444
